TPU v7x, 8 devices: a whole 2x2x1 slice. The times are simulated.
8 devices in a mesh: dp: 1 (over z), tp2: 2 (over y), tp: 4 (over x, core).
Axes of the slice: x: 2, y: 2, z: 1, core: 2. Of those that a mesh axis runs over, the one named last changes fastest.
Arguments:
- attn_out: bfloat16 [4096, 16384], P('dp', 'tp')
- w_out: bfloat16 [16384, 16384], P('tp', 'tp2')
- residual: bfloat16 [4096, 16384], P(('dp', 'tp'), 'tp2')
- norm_gain: float32 [16384], P('tp2')
Outputs:
- output 1: bfloat16 [4096, 16384], P(('dp', 'tp'), 'tp2')
- output 2: bfloat16 [4096, 16384], P(('dp', 'tp'), 'tp2')
All inputs are finite; a program needn't handle non-finite values.
Results may differ from a plain program's by a relative error of at most 0.00721035.
Values are sent between devices in bfloat16 or wider.
A program may use at most 1 GiB of HBM per device.

v0:
```python
import jax
import jax.numpy as jnp
from jax import lax
from jax.sharding import PartitionSpec as P, NamedSharding

EPS_NORM = 1e-6


def solution(mesh):
    tp_size = mesh.shape["tp"]
    col_groups = mesh.shape["tp2"]

    def local_step(attn_blk, w_blk, res_blk, gain_blk):
        block_prod = jnp.dot(attn_blk, w_blk, preferred_element_type=jnp.float32).astype(jnp.bfloat16)
        token_rows, local_cols = block_prod.shape
        received = lax.all_to_all(block_prod, "tp", 0, 0, tiled=True)
        y_sum = jnp.sum(received.reshape(tp_size, token_rows // tp_size, local_cols), axis=0, dtype=jnp.float32)
        hidden = res_blk.astype(jnp.float32) + y_sum
        sq_sum = lax.psum(jnp.sum(hidden * hidden, axis=-1, keepdims=True), "tp2")
        inv_rms = lax.rsqrt(sq_sum / (local_cols * col_groups) + EPS_NORM)
        normed = hidden * inv_rms * gain_blk
        return hidden.astype(jnp.bfloat16), normed.astype(jnp.bfloat16)

    row_spec = P(("dp", "tp"), "tp2")
    return jax.shard_map(local_step, mesh=mesh, in_specs=(P("dp", "tp"), P("tp", "tp2"), row_spec, P("tp2")), out_specs=(row_spec, row_spec), check_vma=False)
```

profile of v0, /device:TPU:0, one launch (start us, length us, event | category | flops | bytes accessed | tf_op | source)
XLA Modules:
  0.0 1144.8 jit_solution(12205326409496133497)
XLA Ops:
  0.6 292.4 %convolution_convert_fusion = bf16[4096,8192]{1,0:T(8,128)(2,1)} fusion(bf16[4096,4096]{1,0:T(8,128)(2,1)} %param.4, bf16[4096,8192]{1,0:T(8,128)(2,1)} %param.5), kind=kOutput, calls=%fused_computation.1 | convolution fusion | flops 274911461376 | bytes 167772160 | tf_op jit(solution)/shard_map/dot_general | solution.py:14
  293.1 755.5 %all_to_all.9 = bf16[4,1024,8192]{2,1,0:T(8,128)(2,1)} all-to-all(bf16[4,1024,8192]{2,1,0:T(8,128)(2,1)} %bitcast), channel_id=1, replica_groups=mesh['dp'=1,'tp2'=2,'tp'=4] {'tp'}, dimensions={0} | all-to-all | bytes 134217728 | tf_op jit(solution)/shard_map/all_to_all | solution.py:16
  1048.6 47.3 %convert_reduce_fusion = f32[1024,8192]{1,0:T(8,128)} fusion(bf16[4,1024,8192]{2,1,0:T(8,128)(2,1)} %all_to_all.9), kind=kLoop, calls=%fused_computation | loop fusion | flops 58720256 | bytes 100663296 | tf_op jit(solution)/shard_map/reduce_sum | solution.py:17
  1095.9 0.0 copy-start
  1095.9 16.4 %multiply_reduce_fusion = f32[1024]{0:T(1024)S(1)} fusion(f32[1024,8192]{1,0:T(8,128)} %convert_reduce_fusion, bf16[1024,8192]{1,0:T(8,128)(2,1)} %param.6), kind=kLoop, calls=%fused_computation.3 | loop fusion | flops 33553408 | bytes 50335744 | tf_op jit(solution)/shard_map/reduce_sum | solution.py:19
  1112.3 5.1 psum.7
  1117.5 0.0 copy-done
  1117.5 27.3 %multiply_convert_fusion = (bf16[1024,8192]{1,0:T(8,128)(2,1)}, bf16[1024,8192]{1,0:T(8,128)(2,1)}) fusion(f32[8192]{0:T(1024)S(1)} %copy-done, f32[1024]{0:T(1024)S(1)} %bitcast.5, f32[1024,8192]{1,0:T(8,128)} %convert_reduce_fusion, bf16[1024,8192]{1,0:T(8,128)(2,1)} %param.6), kind=kLoop, calls=%fused_computation.2 | loop fusion | flops 50331648 | bytes 83922944 | tf_op jit(solution)/shard_map/convert_element_type | solution.py:22
  (1 shorter events, 0.0 us)
Async XLA Ops:
  1095.9 21.6 %copy-start = (f32[8192]{0:T(1024)S(1)}, f32[8192]{0:T(1024)}, u32[]{:S(2)}) copy-start(f32[8192]{0:T(1024)} %param.7) | copy-start | bytes 98308
where the time goes:
time: 1150 us; the launch traced here: 1140 us
  blocking collectives  761 us (66%)
  matrix products  292 us (25%)
  other arithmetic  91 us (8%)
    all_to_all x1, blocking collectives, local_step(): received = lax.all_to_all(block_prod, 'tp', 0, 0, tiled=True)  756 us
    dot_general x1, matrix products, local_step(): jnp.dot(attn_blk, w_blk, preferred_element_type=jnp.float32)  292 us
    reduce_sum x1, other arithmetic, local_step(): jnp.sum(received.reshape(tp_size, token_rows // tp_size, local_cols), axi...  47.3 us
    convert_element_type x1, other arithmetic, local_step(): return (hidden.astype(jnp.bfloat16), normed.astype(jnp.bfloat16))  27.3 us

commit v1 on v0

v1 whole, which is shorter than its diff:
```python
import jax
import jax.numpy as jnp
from jax import lax
from jax.experimental import pallas as pl
from jax.experimental.pallas import tpu as pltpu
from jax.sharding import PartitionSpec as P


EPS_NORM = 1e-6
F32, BF16 = jnp.float32, jnp.bfloat16
VMEM_BYTES = 67043328

ANY = pl.BlockSpec(memory_space=pl.ANY)
PARAMS = pltpu.CompilerParams(vmem_limit_bytes=VMEM_BYTES)


def products(attn, w, blocks, reps, tm, col0, ncols, tn, splits, deps):
    depth = attn.shape[1]
    nb, ns = len(blocks), len(splits)
    index = jnp.stack(blocks).astype(jnp.int32)

    def body(index_ref, *refs):
        a_refs, w_ref = refs[:nb], refs[nb]
        outs = refs[nb + 1 + len(deps):]
        for b in range(nb):
            val = jnp.dot(a_refs[b][...], w_ref[...], preferred_element_type=F32).astype(BF16)
            row = 0
            for s, size in enumerate(splits):
                outs[b * ns + s][...] = val[row:row + size]
                row += size

    c0 = col0 // tn
    a_specs = [pl.BlockSpec((tm, depth), lambda j, i, idx, b=b: (idx[b] + i, 0)) for b in range(nb)]
    w_spec = pl.BlockSpec((depth, tn), lambda j, i, idx: (0, c0 + j))
    out_specs = [pl.BlockSpec((size, tn), lambda j, i, idx: (i, j)) for _ in range(nb) for size in splits]
    return pl.pallas_call(
        body,
        grid_spec=pltpu.PrefetchScalarGridSpec(
            num_scalar_prefetch=1,
            grid=(ncols // tn, reps),
            in_specs=a_specs + [w_spec] + [ANY] * len(deps),
            out_specs=out_specs,
        ),
        out_shape=[jax.ShapeDtypeStruct((size * reps, ncols), BF16) for _ in range(nb) for size in splits],
        compiler_params=PARAMS,
        cost_estimate=pl.CostEstimate(
            flops=2 * nb * reps * tm * depth * ncols,
            bytes_accessed=2 * (depth * ncols + nb * reps * tm * (depth + ncols)),
            transcendentals=0),
    )(index, *([attn] * nb), w, *deps)


def add_rows(res, near, far, row0, rows, tr, state, deps):
    total_rows, cols = res.shape
    nn, nf, per = len(near), len(far), len(far[0])
    widths = [piece.shape[1] for piece in far[0]]
    flat = [piece for group in far for piece in group]

    def body(*refs):
        r_ref, near_refs, far_refs = refs[0], refs[1:1 + nn], refs[1 + nn:1 + nn + nf * per]
        h_ref, ho_ref, sq_ref = refs[-3:]
        total = jnp.zeros((tr, 1), F32)
        base = 0
        for c, width in enumerate(widths):
            sl = slice(base, base + width)
            y = near_refs[0][:, sl].astype(F32)
            for ref in near_refs[1:]:
                y = y + ref[:, sl].astype(F32)
            for g in range(nf):
                y = y + far_refs[g * per + c][...].astype(F32)
            h = r_ref[:, sl].astype(F32) + y
            h_ref[:, sl] = h
            ho_ref[:, sl] = h.astype(BF16)
            total = total + jnp.sum(h * h, axis=-1, keepdims=True)
            base += width
        sq_ref[...] = total

    b0 = row0 // tr
    full = pl.BlockSpec((tr, cols), lambda i: (b0 + i, 0))
    in_specs = [full] * (1 + nn) + [pl.BlockSpec((tr, piece.shape[1]), lambda i: (i, 0)) for piece in flat]
    args = [res, *near, *flat]
    in_specs += [ANY] * (len(deps) + len(state))
    args += [*deps, *state]
    first = len(args) - len(state)
    return pl.pallas_call(
        body,
        grid=(rows // tr,),
        in_specs=in_specs,
        out_specs=[full, full, pl.BlockSpec((tr, 1), lambda i: (b0 + i, 0))],
        out_shape=[
            jax.ShapeDtypeStruct((total_rows, cols), F32),
            jax.ShapeDtypeStruct((total_rows, cols), BF16),
            jax.ShapeDtypeStruct((total_rows, 1), F32),
        ],
        input_output_aliases={first + i: i for i in range(len(state))},
        compiler_params=PARAMS,
        cost_estimate=pl.CostEstimate(flops=8 * rows * cols, bytes_accessed=16 * rows * cols, transcendentals=0),
    )(*args)


def norm_rows(h, sq, gain, width, row0, rows, sq_row0, tr, n_out):
    total_rows, cols = h.shape

    def body(*refs):
        h_ref, sq_ref, g_ref, n_ref = refs[0], refs[1], refs[2], refs[-1]
        inv = lax.rsqrt(sq_ref[...] / width + EPS_NORM)
        n_ref[...] = (h_ref[...] * inv * g_ref[...]).astype(BF16)

    b0, s0 = row0 // tr, sq_row0 // tr
    in_specs = [
        pl.BlockSpec((tr, cols), lambda i: (b0 + i, 0)),
        pl.BlockSpec((tr, 1), lambda i: (s0 + i, 0)),
        pl.BlockSpec((1, cols), lambda i: (0, 0)),
    ]
    args = [h, sq, gain]
    if n_out is not None:
        in_specs.append(ANY)
        args.append(n_out)
    return pl.pallas_call(
        body,
        grid=(rows // tr,),
        in_specs=in_specs,
        out_specs=pl.BlockSpec((tr, cols), lambda i: (b0 + i, 0)),
        out_shape=jax.ShapeDtypeStruct((total_rows, cols), BF16),
        input_output_aliases={} if n_out is None else {3: 0},
        compiler_params=PARAMS,
        cost_estimate=pl.CostEstimate(flops=4 * rows * cols, bytes_accessed=6 * rows * cols, transcendentals=0),
    )(*args)


TM = 256
FIRST_COLS = (512, 1536, 6144)
LAST_ROWS = (128, 64, 64)


def solution(mesh):
    tp = mesh.shape["tp"]
    col_groups = mesh.shape["tp2"]

    def send(x, flip):
        return lax.ppermute(x, "tp", [(i, i ^ flip) for i in range(tp)])

    def inner(attn, w, res, gain):
        me = lax.axis_index("tp")
        rows_total, cols = res.shape
        per = rows_total // TM
        plan, col0 = [], 0
        for ncols in FIRST_COLS:
            plan.append((0, col0, ncols, 512, (TM,)))
            col0 += ncols
        plan += [(k, 0, cols, 512, (TM,)) for k in range(1, per - 1)]
        plan += [(per - 1, 0, cols, 512, LAST_ROWS)]
        near_at = len(FIRST_COLS) + 1
        pieces = {}
        dep = []
        near = None

        for t, (k, col0, ncols, tn, splits) in enumerate(plan):
            if t == near_at:
                other, own = products(attn, w, [(me ^ 1) * per, me * per], per, TM, 0, cols, 1024, (TM,), dep)
                dep = [own]
                near = [own, send(other, 1)]
            outs = products(attn, w, [(me ^ 2) * per + k, (me ^ 3) * per + k], 1, TM, col0, ncols, tn, splits, dep)
            dep = [outs[0]]
            row = k * TM
            for s, size in enumerate(splits):
                got = pieces.setdefault((row, size), ([], []))
                for b, flip in enumerate((2, 3)):
                    got[b].append(send(outs[b * len(splits) + s], flip))
                row += size

        chunks = sorted(pieces)
        gain2 = gain.reshape(1, cols)
        state = []
        for c, (row, size) in enumerate(chunks[:-1]):
            state = add_rows(res, near, pieces[row, size], row, size, 64, state, dep if c == 0 else [])
        last, last_size = chunks[-1]
        h, h_out, sq = state
        sq_a = lax.psum(sq, "tp2")
        n_out = norm_rows(h, sq_a, gain2, cols * col_groups, 0, last, 0, 64, None)
        h, h_out, sq = add_rows(res, near, pieces[last, last_size], last, last_size, last_size, state, [n_out])
        sq_b = lax.psum(sq[last:], "tp2")
        n_out = norm_rows(h, sq_b, gain2, cols * col_groups, last, last_size, 0, last_size, n_out)
        return h_out, n_out

    row_spec = P(("dp", "tp"), "tp2")
    fn = jax.shard_map(inner, mesh=mesh, in_specs=(P("dp", "tp"), P("tp", "tp2"), row_spec, P("tp2")), out_specs=(row_spec, row_spec), check_vma=False)
    shapes = [jax.ShapeDtypeStruct(s, d) for s, d in (((4096, 16384), BF16), ((16384, 16384), BF16), ((4096, 16384), BF16), ((16384,), F32))]
    jax.eval_shape(fn, *shapes)
    return fn
```

time: 1150 us -> 1000 us (0.87)
  blocking collectives: 761 us -> 27.4 us
  waiting for transfers between devices: 0 us -> 534 us
  Pallas kernels: 0 us -> 414 us
  matrix products: 292 us -> 0 us
  other arithmetic: 91 us -> 2.94 us
  starting transfers between devices: 0 us -> 17.5 us
    all_to_all x1 -> x0, blocking collectives: 756 us -> none  [local_step(): received = lax.all_to_all(block_prod, 'tp', 0, 0, tiled=True)]
    ppermute x0 -> x17, waiting for transfers between devices: none -> 534 us  [send(): return lax.ppermute(x, 'tp', [(i, i ^ flip) for i in range(tp)])]
    pallas_call x0 -> x15, Pallas kernels: none -> 414 us  [the longest x7 333 us: products(): pl.pallas_call(body, grid_spec=pltpu.PrefetchScalarGridSpec(num_scalar_pr...]
    dot_general x1 -> x0, matrix products: 292 us -> none  [local_step(): jnp.dot(attn_blk, w_blk, preferred_element_type=jnp.float32)]
    reduce_sum x2 -> x0, other arithmetic: 63.7 us -> none  [the longest x1 47.3 us: local_step(): jnp.sum(received.reshape(tp_size, token_rows // tp_size, local_cols), axi...]
    convert_element_type x1 -> x0, other arithmetic: 27.3 us -> none  [local_step(): return (hidden.astype(jnp.bfloat16), normed.astype(jnp.bfloat16))]
    psum x1 -> x2, blocking collectives: 5.14 us -> 27.4 us  [the longest x1 19.4 us: inner(): sq_a = lax.psum(sq, 'tp2')]
    ppermute x0 -> x17, starting transfers between devices: none -> 17.5 us  [send(): return lax.ppermute(x, 'tp', [(i, i ^ flip) for i in range(tp)])]
  transfers between devices with their start and end apart: 0 -> 17, of which waited for: 0 -> 9; matrix products, arithmetic and copies ran while one was open for 0% -> 0% of each run, Pallas kernels for 0% -> 16%
where the time goes in v1:
time: 1000 us; the launch traced here: 998 us
  waiting for transfers between devices  534 us (53%)
  Pallas kernels  414 us (41%)
  blocking collectives  27.4 us (3%)
  starting transfers between devices  17.5 us (2%)
    ppermute x17, waiting for transfers between devices, send(): return lax.ppermute(x, 'tp', [(i, i ^ flip) for i in range(tp)])  534 us
    pallas_call x7, Pallas kernels, products(): pl.pallas_call(body, grid_spec=pltpu.PrefetchScalarGridSpec(num_scalar_pr...  333 us
    pallas_call x6, Pallas kernels, add_rows(): pl.pallas_call(body, grid=(rows // tr,), in_specs=in_specs, out_specs=[fu...  54.5 us
    pallas_call x2, Pallas kernels, norm_rows(): pl.pallas_call(body, grid=(rows // tr,), in_specs=in_specs, out_specs=pl....  26.2 us
  transfers between devices with their start and end apart: 17, of which 9 were waited for; matrix products, arithmetic and copies ran while one was open for 0% of the time, Pallas kernels for 16%

profile of v1, /device:TPU:0, one launch (start us, length us, event | category | flops | bytes accessed | tf_op | source)
XLA Modules:
  0.0 997.5 jit_solution(899023590301458457)
XLA Ops:
  0.6 0.6 pad_add_fusion.2.index_ref
  1.2 7.1 shard_map.59
  8.4 12.0 %shard_map.60 = (bf16[256,1536]{1,0:T(8,128)(2,1)}, bf16[256,1536]{1,0:T(8,128)(2,1)}) custom-call(s32[2]{0:T(128)} %pad_add_fusion.2.index_ref, bf16[4096,4096]{1,0:T(8,128)(2,1)} %refs_1_.13, bf16[4096,4096]{1,0:T(8,128)(2,1)} %refs_1_.13, bf16[4096,8192]{1,0:T(8,128)(2,1)} %refs_2_.13, bf16[256,512]{1,0:T(8,128)(2,1)} %get-tuple-element.38.refs_3_), custom_call_target="tpu_custom_call" | custom-call | flops 6442450944 | bytes 18350080 | tf_op jit(solution)/shard_map/pallas_call | solution.py:36
  20.3 33.2 %shard_map.61 = (bf16[256,6144]{1,0:T(8,128)(2,1)}, bf16[256,6144]{1,0:T(8,128)(2,1)}) custom-call(s32[2]{0:T(128)} %pad_add_fusion.2.index_ref, bf16[4096,4096]{1,0:T(8,128)(2,1)} %refs_1_.13, bf16[4096,4096]{1,0:T(8,128)(2,1)} %refs_1_.13, bf16[4096,8192]{1,0:T(8,128)(2,1)} %refs_2_.13, bf16[256,1536]{1,0:T(8,128)(2,1)} %get-tuple-element.39.refs_3_), custom_call_target="tpu_custom_call" | custom-call | flops 25769803776 | bytes 60817408 | tf_op jit(solution)/shard_map/pallas_call | solution.py:36
  53.6 0.6 pad_add_fusion.index_ref
  54.2 0.6 pad_add_fusion.1.index_ref
  54.7 42.6 %shard_map.62 = (bf16[256,8192]{1,0:T(8,128)(2,1)}, bf16[256,8192]{1,0:T(8,128)(2,1)}) custom-call(s32[2]{0:T(128)} %pad_add_fusion.1.index_ref, bf16[4096,4096]{1,0:T(8,128)(2,1)} %refs_1_.13, bf16[4096,4096]{1,0:T(8,128)(2,1)} %refs_1_.13, bf16[4096,8192]{1,0:T(8,128)(2,1)} %refs_2_.13, bf16[256,6144]{1,0:T(8,128)(2,1)} %get-tuple-element.40.refs_3_), custom_call_target="tpu_custom_call" | custom-call | flops 34359738368 | bytes 79691776 | tf_op jit(solution)/shard_map/pallas_call | solution.py:36
  97.4 153.2 %shard_map.63 = (bf16[1024,8192]{1,0:T(8,128)(2,1)}, bf16[1024,8192]{1,0:T(8,128)(2,1)}) custom-call(s32[2]{0:T(128)} %pad_add_fusion.index_ref, bf16[4096,4096]{1,0:T(8,128)(2,1)} %refs_1_.13, bf16[4096,4096]{1,0:T(8,128)(2,1)} %refs_1_.13, bf16[4096,8192]{1,0:T(8,128)(2,1)} %refs_2_.13, bf16[256,8192]{1,0:T(8,128)(2,1)} %get-tuple-element.41.refs_3_), custom_call_target="tpu_custom_call" | custom-call | flops 137438953472 | bytes 117440512 | tf_op jit(solution)/shard_map/pallas_call | solution.py:36
  250.5 0.8 collective-permute-start
  251.4 2.5 collective-permute-start.11
  253.9 0.0 collective-permute-start.13
  253.9 1.5 collective-permute-start.14
  255.4 0.2 collective-permute-start.15
  255.6 0.6 pad_add_fusion.4.index_ref
  256.2 42.6 %shard_map.64 = (bf16[256,8192]{1,0:T(8,128)(2,1)}, bf16[256,8192]{1,0:T(8,128)(2,1)}) custom-call(s32[2]{0:T(128)} %pad_add_fusion.4.index_ref, bf16[4096,4096]{1,0:T(8,128)(2,1)} %refs_1_.13, bf16[4096,4096]{1,0:T(8,128)(2,1)} %refs_1_.13, bf16[4096,8192]{1,0:T(8,128)(2,1)} %refs_2_.13, bf16[1024,8192]{1,0:T(8,128)(2,1)} %get-tuple-element.42.refs_3_.refs_1_), custom_call_target="tpu_custom_call" | custom-call | flops 34359738368 | bytes 79691776 | tf_op jit(solution)/shard_map/pallas_call | solution.py:36
  298.9 0.6 pad_add_fusion.3.index_ref
  299.5 34.5 %collective-permute-done.14.refs_6_ = bf16[256,512]{1,0:T(8,128)(2,1)} collective-permute-done((bf16[256,512]{1,0:T(8,128)(2,1)}, bf16[256,512]{1,0:T(8,128)(2,1)}, u32[]{:S(2)}, u32[]{:S(2)}) %collective-permute-start.14) | collective-permute-done | bytes 262176 | tf_op jit(solution)/shard_map/ppermute | solution.py:141
  334.0 2.1 collective-permute-start.16
  336.1 42.6 %shard_map.65 = (bf16[128,8192]{1,0:T(8,128)(2,1)}, bf16[64,8192]{1,0:T(8,128)(2,1)}, bf16[64,8192]{1,0:T(8,128)(2,1)}, bf16[128,8192]{1,0:T(8,128)(2,1)}, bf16[...) custom-call(s32[2]{0:T(128)} %pad_add_fusion.3.index_ref, bf16[4096,4096]{1,0:T(8,128)(2,1)} %refs_1_.13, ...), custom_call_target="tpu_custom_call" | custom-call | flops 34359738368 | bytes 79691776 | tf_op jit(solution)/shard_map/pallas_call | solution.py:36
  378.8 1.1 collective-permute-start.12
  379.9 100.4 %collective-permute-done.12.refs_4_ = bf16[256,1536]{1,0:T(8,128)(2,1)} collective-permute-done((bf16[256,1536]{1,0:T(8,128)(2,1)}, bf16[256,1536]{1,0:T(8,128)(2,1)}, u32[]{:S(2)}, u32[]{:S(2)}) %collective-permute-start.12) | collective-permute-done | bytes 786464 | tf_op jit(solution)/shard_map/ppermute | solution.py:141
  480.2 1.0 collective-permute-start.10
  481.2 0.8 collective-permute-start.9
  482.0 1.5 collective-permute-start.8
  483.5 0.3 collective-permute-start.7
  483.8 89.4 %collective-permute-done.10.refs_4_ = bf16[256,8192]{1,0:T(8,128)(2,1)} collective-permute-done((bf16[256,8192]{1,0:T(8,128)(2,1)}, bf16[256,8192]{1,0:T(8,128)(2,1)}, u32[]{:S(2)}, u32[]{:S(2)}) %collective-permute-start.10) | collective-permute-done | bytes 4194336 | tf_op jit(solution)/shard_map/ppermute | solution.py:141
  573.1 2.0 collective-permute-start.5
  575.2 88.4 %collective-permute-done.9.refs_3_ = bf16[256,8192]{1,0:T(8,128)(2,1)} collective-permute-done((bf16[256,8192]{1,0:T(8,128)(2,1)}, bf16[256,8192]{1,0:T(8,128)(2,1)}, u32[]{:S(2)}, u32[]{:S(2)}) %collective-permute-start.9) | collective-permute-done | bytes 4194336 | tf_op jit(solution)/shard_map/ppermute | solution.py:141
  663.6 1.1 collective-permute-start.3
  664.7 88.2 %collective-permute-done.8.refs_4_ = bf16[256,8192]{1,0:T(8,128)(2,1)} collective-permute-done((bf16[256,8192]{1,0:T(8,128)(2,1)}, bf16[256,8192]{1,0:T(8,128)(2,1)}, u32[]{:S(2)}, u32[]{:S(2)}) %collective-permute-start.8) | collective-permute-done | bytes 4194336 | tf_op jit(solution)/shard_map/ppermute | solution.py:141
  752.9 1.4 collective-permute-start.4
  754.3 89.1 %collective-permute-done.7.refs_3_ = bf16[256,8192]{1,0:T(8,128)(2,1)} collective-permute-done((bf16[256,8192]{1,0:T(8,128)(2,1)}, bf16[256,8192]{1,0:T(8,128)(2,1)}, u32[]{:S(2)}, u32[]{:S(2)}) %collective-permute-start.7) | collective-permute-done | bytes 4194336 | tf_op jit(solution)/shard_map/ppermute | solution.py:141
  843.4 1.1 collective-permute-start.1
  844.5 0.1 collective-permute-start.2
  844.5 12.2 %shard_map.66 = (f32[1024,8192]{1,0:T(8,128)}, bf16[1024,8192]{1,0:T(8,128)(2,1)}, f32[1024,1]{1,0:T(8,128)}) custom-call(bf16[1024,8192]{1,0:T(8,128)(2,1)} %refs_0_.25, bf16[1024,8192]{1,0:T(8,128)(2,1)} %get-tuple-element.42.refs_3_.refs_1_, bf16[1024,8192]{1,0:T(8,128)(2,1)} %collective-permute-done.refs_2_, ...), custom_call_target="tpu_custom_call" | custom-call | flops 16777216 | bytes 33554432 | tf_op jit(solution)/shard_map/pallas_call | solution.py:85
  856.8 12.5 %shard_map.67 = (f32[1024,8192]{1,0:T(8,128)}, bf16[1024,8192]{1,0:T(8,128)(2,1)}, f32[1024,1]{1,0:T(8,128)}) custom-call(bf16[1024,8192]{1,0:T(8,128)(2,1)} %refs_0_.25, bf16[1024,8192]{1,0:T(8,128)(2,1)} %get-tuple-element.42.refs_3_.refs_1_, ...), custom_call_target="tpu_custom_call", output_to_operand_aliasing={{0}: (5, {}), {1}: (6, {}), {2}: (7, {})} | custom-call | flops 16777216 | bytes 33554432 | tf_op jit(solution)/shard_map/pallas_call | solution.py:85
  869.3 12.4 %shard_map.68 = (f32[1024,8192]{1,0:T(8,128)}, bf16[1024,8192]{1,0:T(8,128)(2,1)}, f32[1024,1]{1,0:T(8,128)}) custom-call(bf16[1024,8192]{1,0:T(8,128)(2,1)} %refs_0_.25, bf16[1024,8192]{1,0:T(8,128)(2,1)} %get-tuple-element.42.refs_3_.refs_1_, ...), custom_call_target="tpu_custom_call", output_to_operand_aliasing={{0}: (5, {}), {1}: (6, {}), {2}: (7, {})} | custom-call | flops 16777216 | bytes 33554432 | tf_op jit(solution)/shard_map/pallas_call | solution.py:85
  881.7 6.6 collective-permute-done.5.refs_3_
  888.3 6.8 shard_map.69
  895.1 15.7 %collective-permute-done.3.refs_3_ = bf16[64,8192]{1,0:T(8,128)(2,1)} collective-permute-done((bf16[64,8192]{1,0:T(8,128)(2,1)}, bf16[64,8192]{1,0:T(8,128)(2,1)}, u32[]{:S(2)}, u32[]{:S(2)}) %collective-permute-start.3) | collective-permute-done | bytes 1048608 | tf_op jit(solution)/shard_map/ppermute | solution.py:141
  910.8 21.9 %collective-permute-done.4.refs_4_ = bf16[64,8192]{1,0:T(8,128)(2,1)} collective-permute-done((bf16[64,8192]{1,0:T(8,128)(2,1)}, bf16[64,8192]{1,0:T(8,128)(2,1)}, u32[]{:S(2)}, u32[]{:S(2)}) %collective-permute-start.4) | collective-permute-done | bytes 1048608 | tf_op jit(solution)/shard_map/ppermute | solution.py:141
  932.7 5.3 shard_map.70
  937.9 19.4 %psum.14.refs_1_ = f32[1024,1]{1,0:T(8,128)} all-reduce(f32[1024,1]{1,0:T(8,128)} %get-tuple-element.69.refs_8_), channel_id=1, replica_groups=mesh['dp'=1,'tp2'=2,'tp'=4] {'tp2'}, use_global_device_ids=true, to_apply=%region_0.0 | all-reduce | flops 1024 | bytes 8192 | tf_op jit(solution)/shard_map/psum | solution.py:179
  957.3 23.1 %shard_map.71.refs_5_.refs_3_ = bf16[1024,8192]{1,0:T(8,128)(2,1)} custom-call(f32[1024,8192]{1,0:T(8,128)} %get-tuple-element.68.refs_0_.refs_6_, f32[1024,1]{1,0:T(8,128)} %psum.14.refs_1_, f32[1,8192]{1,0:T(1,128)} %bitcast.11), custom_call_target="tpu_custom_call" | custom-call | flops 31457280 | bytes 47185920 | tf_op jit(solution)/shard_map/pallas_call | solution.py:119
  980.4 5.3 shard_map.72
  985.7 0.8 slice.3
  986.5 8.0 psum.15.refs_1_
  994.5 3.0 shard_map.73
  (9 shorter events, 0.0 us)
Async XLA Ops:
  250.5 593.9 %collective-permute-start = (bf16[1024,8192]{1,0:T(8,128)(2,1)}, bf16[1024,8192]{1,0:T(8,128)(2,1)}, u32[]{:S(2)}, u32[]{:S(2)}) collective-permute-start(bf16[1024,8192]{1,0:T(8,128)(2,1)} %get-tuple-element.43), channel_id=1, source_target_pairs={{0,1},{1,0},{2,3},{3,2},{4,5},{5,4},{6,7},{7,6}} | collective-permute-start | bytes 50331656 | tf_op jit(solution)/shard_map/ppermute | solution.py:141
  251.4 127.3 %collective-permute-start.11 = (bf16[256,512]{1,0:T(8,128)(2,1)}, bf16[256,512]{1,0:T(8,128)(2,1)}, u32[]{:S(2)}, u32[]{:S(2)}) collective-permute-start(bf16[256,512]{1,0:T(8,128)(2,1)} %get-tuple-element.38.refs_3_), channel_id=1, source_target_pairs={{0,2},{1,3},{2,0},{3,1},{4,6},{5,7},{6,4},{7,5}} | collective-permute-start | bytes 786440 | tf_op jit(solution)/shard_map/ppermute | solution.py:141
  253.9 229.6 %collective-permute-start.13 = (bf16[256,6144]{1,0:T(8,128)(2,1)}, bf16[256,6144]{1,0:T(8,128)(2,1)}, u32[]{:S(2)}, u32[]{:S(2)}) collective-permute-start(bf16[256,6144]{1,0:T(8,128)(2,1)} %get-tuple-element.40.refs_3_), channel_id=1, source_target_pairs={{0,2},{1,3},{2,0},{3,1},{4,6},{5,7},{6,4},{7,5}} | collective-permute-start | bytes 9437192 | tf_op jit(solution)/shard_map/ppermute | solution.py:141
  253.9 80.1 %collective-permute-start.14 = (bf16[256,512]{1,0:T(8,128)(2,1)}, bf16[256,512]{1,0:T(8,128)(2,1)}, u32[]{:S(2)}, u32[]{:S(2)}) collective-permute-start(bf16[256,512]{1,0:T(8,128)(2,1)} %get-tuple-element.53), channel_id=1, source_target_pairs={{0,3},{1,2},{2,1},{3,0},{4,7},{5,6},{6,5},{7,4}} | collective-permute-start | bytes 786440 | tf_op jit(solution)/shard_map/ppermute | solution.py:141
  255.4 123.3 %collective-permute-start.15 = (bf16[256,1536]{1,0:T(8,128)(2,1)}, bf16[256,1536]{1,0:T(8,128)(2,1)}, u32[]{:S(2)}, u32[]{:S(2)}) collective-permute-start(bf16[256,1536]{1,0:T(8,128)(2,1)} %get-tuple-element.54), channel_id=1, source_target_pairs={{0,3},{1,2},{2,1},{3,0},{4,7},{5,6},{6,5},{7,4}} | collective-permute-start | bytes 2359304 | tf_op jit(solution)/shard_map/ppermute | solution.py:141
  334.0 148.0 %collective-permute-start.16 = (bf16[256,6144]{1,0:T(8,128)(2,1)}, bf16[256,6144]{1,0:T(8,128)(2,1)}, u32[]{:S(2)}, u32[]{:S(2)}) collective-permute-start(bf16[256,6144]{1,0:T(8,128)(2,1)} %get-tuple-element.55), channel_id=1, source_target_pairs={{0,3},{1,2},{2,1},{3,0},{4,7},{5,6},{6,5},{7,4}} | collective-permute-start | bytes 9437192 | tf_op jit(solution)/shard_map/ppermute | solution.py:141
  378.7 102.5 %collective-permute-start.6 = (bf16[128,8192]{1,0:T(8,128)(2,1)}, bf16[128,8192]{1,0:T(8,128)(2,1)}, u32[]{:S(2)}, u32[]{:S(2)}) collective-permute-start(bf16[128,8192]{1,0:T(8,128)(2,1)} %get-tuple-element.50), channel_id=1, source_target_pairs={{0,3},{1,2},{2,1},{3,0},{4,7},{5,6},{6,5},{7,4}} | collective-permute-start | bytes 6291464 | tf_op jit(solution)/shard_map/ppermute | solution.py:141
  378.8 101.5 %collective-permute-start.12 = (bf16[256,1536]{1,0:T(8,128)(2,1)}, bf16[256,1536]{1,0:T(8,128)(2,1)}, u32[]{:S(2)}, u32[]{:S(2)}) collective-permute-start(bf16[256,1536]{1,0:T(8,128)(2,1)} %get-tuple-element.39.refs_3_), channel_id=1, source_target_pairs={{0,2},{1,3},{2,0},{3,1},{4,6},{5,7},{6,4},{7,5}} | collective-permute-start | bytes 2359304 | tf_op jit(solution)/shard_map/ppermute | solution.py:141
  480.2 92.9 %collective-permute-start.10 = (bf16[256,8192]{1,0:T(8,128)(2,1)}, bf16[256,8192]{1,0:T(8,128)(2,1)}, u32[]{:S(2)}, u32[]{:S(2)}) collective-permute-start(bf16[256,8192]{1,0:T(8,128)(2,1)} %get-tuple-element.52), channel_id=1, source_target_pairs={{0,3},{1,2},{2,1},{3,0},{4,7},{5,6},{6,5},{7,4}} | collective-permute-start | bytes 12582920 | tf_op jit(solution)/shard_map/ppermute | solution.py:141
  481.2 182.4 %collective-permute-start.9 = (bf16[256,8192]{1,0:T(8,128)(2,1)}, bf16[256,8192]{1,0:T(8,128)(2,1)}, u32[]{:S(2)}, u32[]{:S(2)}) collective-permute-start(bf16[256,8192]{1,0:T(8,128)(2,1)} %get-tuple-element.41.refs_3_), channel_id=1, source_target_pairs={{0,2},{1,3},{2,0},{3,1},{4,6},{5,7},{6,4},{7,5}} | collective-permute-start | bytes 12582920 | tf_op jit(solution)/shard_map/ppermute | solution.py:141
  482.0 270.9 %collective-permute-start.8 = (bf16[256,8192]{1,0:T(8,128)(2,1)}, bf16[256,8192]{1,0:T(8,128)(2,1)}, u32[]{:S(2)}, u32[]{:S(2)}) collective-permute-start(bf16[256,8192]{1,0:T(8,128)(2,1)} %get-tuple-element.51), channel_id=1, source_target_pairs={{0,3},{1,2},{2,1},{3,0},{4,7},{5,6},{6,5},{7,4}} | collective-permute-start | bytes 12582920 | tf_op jit(solution)/shard_map/ppermute | solution.py:141
  483.5 359.9 %collective-permute-start.7 = (bf16[256,8192]{1,0:T(8,128)(2,1)}, bf16[256,8192]{1,0:T(8,128)(2,1)}, u32[]{:S(2)}, u32[]{:S(2)}) collective-permute-start(bf16[256,8192]{1,0:T(8,128)(2,1)} %get-tuple-element.44.refs_3_), channel_id=1, source_target_pairs={{0,2},{1,3},{2,0},{3,1},{4,6},{5,7},{6,4},{7,5}} | collective-permute-start | bytes 12582920 | tf_op jit(solution)/shard_map/ppermute | solution.py:141
  573.1 315.2 %collective-permute-start.5 = (bf16[128,8192]{1,0:T(8,128)(2,1)}, bf16[128,8192]{1,0:T(8,128)(2,1)}, u32[]{:S(2)}, u32[]{:S(2)}) collective-permute-start(bf16[128,8192]{1,0:T(8,128)(2,1)} %get-tuple-element.49.refs_9_), channel_id=1, source_target_pairs={{0,2},{1,3},{2,0},{3,1},{4,6},{5,7},{6,4},{7,5}} | collective-permute-start | bytes 6291464 | tf_op jit(solution)/shard_map/ppermute | solution.py:141
  663.6 247.2 %collective-permute-start.3 = (bf16[64,8192]{1,0:T(8,128)(2,1)}, bf16[64,8192]{1,0:T(8,128)(2,1)}, u32[]{:S(2)}, u32[]{:S(2)}) collective-permute-start(bf16[64,8192]{1,0:T(8,128)(2,1)} %get-tuple-element.47), channel_id=1, source_target_pairs={{0,2},{1,3},{2,0},{3,1},{4,6},{5,7},{6,4},{7,5}} | collective-permute-start | bytes 3145736 | tf_op jit(solution)/shard_map/ppermute | solution.py:141
  752.9 179.8 %collective-permute-start.4 = (bf16[64,8192]{1,0:T(8,128)(2,1)}, bf16[64,8192]{1,0:T(8,128)(2,1)}, u32[]{:S(2)}, u32[]{:S(2)}) collective-permute-start(bf16[64,8192]{1,0:T(8,128)(2,1)} %get-tuple-element.48), channel_id=1, source_target_pairs={{0,3},{1,2},{2,1},{3,0},{4,7},{5,6},{6,5},{7,4}} | collective-permute-start | bytes 3145736 | tf_op jit(solution)/shard_map/ppermute | solution.py:141
  843.4 137.1 %collective-permute-start.1 = (bf16[64,8192]{1,0:T(8,128)(2,1)}, bf16[64,8192]{1,0:T(8,128)(2,1)}, u32[]{:S(2)}, u32[]{:S(2)}) collective-permute-start(bf16[64,8192]{1,0:T(8,128)(2,1)} %get-tuple-element.45), channel_id=1, source_target_pairs={{0,2},{1,3},{2,0},{3,1},{4,6},{5,7},{6,4},{7,5}} | collective-permute-start | bytes 3145736 | tf_op jit(solution)/shard_map/ppermute | solution.py:141
  844.5 136.0 %collective-permute-start.2 = (bf16[64,8192]{1,0:T(8,128)(2,1)}, bf16[64,8192]{1,0:T(8,128)(2,1)}, u32[]{:S(2)}, u32[]{:S(2)}) collective-permute-start(bf16[64,8192]{1,0:T(8,128)(2,1)} %get-tuple-element.46), channel_id=1, source_target_pairs={{0,3},{1,2},{2,1},{3,0},{4,7},{5,6},{6,5},{7,4}} | collective-permute-start | bytes 3145736 | tf_op jit(solution)/shard_map/ppermute | solution.py:141

commit v2 on v1

v2 whole, which is shorter than its diff:
```python
import jax
import jax.numpy as jnp
from jax import lax
from jax.experimental import pallas as pl
from jax.experimental.pallas import tpu as pltpu
from jax.sharding import PartitionSpec as P


EPS_NORM = 1e-6
F32, BF16 = jnp.float32, jnp.bfloat16
VMEM_BYTES = 67043328

ANY = pl.BlockSpec(memory_space=pl.ANY)
PARAMS = pltpu.CompilerParams(vmem_limit_bytes=VMEM_BYTES)

PLAN = (
    (0, 128, 0, 512, 256, (128,)),
    (0, 128, 512, 1024, 256, (128,)),
    (0, 128, 1536, 2560, 512, (128,)),
    (0, 128, 4096, 4096, 512, (128,)),
    (128, 128, 0, 8192, 512, (128,)),
    (256, 256, 0, 8192, 512, (256,)),
    (512, 256, 0, 8192, 512, (256,)),
    (768, 256, 0, 8192, 512, (128, 96, 32)),
)
NEAR_AT = 6
NEAR_ROWS = 256


def products(attn, w, blocks, reps, tm, col0, ncols, tn, splits, deps):
    depth = attn.shape[1]
    nb, ns = len(blocks), len(splits)

    def body(*refs):
        a_refs, w_ref = refs[nb:2 * nb], refs[2 * nb]
        outs = refs[2 * nb + 1 + len(deps):]
        for b in range(nb):
            val = jnp.dot(a_refs[b][...], w_ref[...], preferred_element_type=F32).astype(BF16)
            row = 0
            for s, size in enumerate(splits):
                outs[b * ns + s][...] = val[row:row + size]
                row += size

    c0 = col0 // tn
    a_specs = [pl.BlockSpec((tm, depth), lambda j, i, *idx, b=b: (idx[b][0] + i, 0)) for b in range(nb)]
    w_spec = pl.BlockSpec((depth, tn), lambda j, i, *idx: (0, c0 + j))
    out_specs = [pl.BlockSpec((size, tn), lambda j, i, *idx: (i, j)) for _ in range(nb) for size in splits]
    return pl.pallas_call(
        body,
        grid_spec=pltpu.PrefetchScalarGridSpec(
            num_scalar_prefetch=nb,
            grid=(ncols // tn, reps),
            in_specs=a_specs + [w_spec] + [ANY] * len(deps),
            out_specs=out_specs,
        ),
        out_shape=[jax.ShapeDtypeStruct((size * reps, ncols), BF16) for _ in range(nb) for size in splits],
        compiler_params=PARAMS,
        cost_estimate=pl.CostEstimate(
            flops=2 * nb * reps * tm * depth * ncols,
            bytes_accessed=2 * (depth * ncols + nb * reps * tm * (depth + ncols)),
            transcendentals=0),
    )(*[b.reshape(1).astype(jnp.int32) for b in blocks], *([attn] * nb), w, *deps)


def add_rows(res, near, far, row0, rows, tr, peers, deps, collective_id):
    cols = res.shape[1]
    nn, nf, per = len(near), len(far), len(far[0])
    widths = [piece.shape[1] for piece in far[0]]
    flat = [piece for group in far for piece in group]
    steps = rows // tr

    def body(*refs):
        r_ref, near_refs, far_refs = refs[0], refs[1:1 + nn], refs[1 + nn:1 + nn + nf * per]
        h_ref, sq_ref, mine, theirs, send_sem, recv_sem = refs[-6:]
        i = pl.program_id(0)
        peer = {"tp2": peers - 1 - lax.axis_index("tp2")}
        barrier = pltpu.get_barrier_semaphore()

        @pl.when(i == 0)
        def _():
            pl.semaphore_signal(barrier, inc=1, device_id=peer, device_id_type=pl.DeviceIdType.MESH)

        total = jnp.zeros((tr, 1), F32)
        base = 0
        for c, width in enumerate(widths):
            sl = slice(base, base + width)
            y = near_refs[0][:, sl].astype(F32)
            for ref in near_refs[1:]:
                y = y + ref[:, sl].astype(F32)
            for g in range(nf):
                y = y + far_refs[g * per + c][...].astype(F32)
            h = r_ref[:, sl].astype(F32) + y
            h_ref[:, sl] = h
            total = total + jnp.sum(h * h, axis=-1, keepdims=True)
            base += width
        mine[pl.ds(pl.multiple_of(i * tr, tr), tr), :] = jnp.broadcast_to(total, (tr, 128))

        @pl.when(i == steps - 1)
        def _():
            pl.semaphore_wait(barrier, 1)
            copy = pltpu.make_async_remote_copy(
                src_ref=mine, dst_ref=theirs, send_sem=send_sem, recv_sem=recv_sem,
                device_id=peer, device_id_type=pl.DeviceIdType.MESH)
            copy.start()
            copy.wait()
            sq_ref[...] = mine[...] + theirs[...]

    b0 = row0 // tr
    full = pl.BlockSpec((tr, cols), lambda i: (b0 + i, 0))
    in_specs = [full] * (1 + nn) + [pl.BlockSpec((tr, piece.shape[1]), lambda i: (i, 0)) for piece in flat] + [ANY] * len(deps)
    return pl.pallas_call(
        body,
        grid=(steps,),
        in_specs=in_specs,
        out_specs=[pl.BlockSpec((tr, cols), lambda i: (i, 0)), pl.BlockSpec((rows, 128), lambda i: (0, 0))],
        out_shape=[jax.ShapeDtypeStruct((rows, cols), F32), jax.ShapeDtypeStruct((rows, 128), F32)],
        scratch_shapes=[
            pltpu.VMEM((rows, 128), F32),
            pltpu.VMEM((rows, 128), F32),
            pltpu.SemaphoreType.DMA,
            pltpu.SemaphoreType.DMA,
        ],
        compiler_params=pltpu.CompilerParams(vmem_limit_bytes=VMEM_BYTES, collective_id=collective_id, has_side_effects=True),
        cost_estimate=pl.CostEstimate(flops=8 * rows * cols, bytes_accessed=14 * rows * cols, transcendentals=0),
    )(res, *near, *flat, *deps)


def norm_rows(h, sq, gain, width, total_rows, row0, tr, state):
    rows, cols = h.shape

    def body(*refs):
        h_ref, sq_ref, g_ref, ho_ref, n_ref = refs[0], refs[1], refs[2], refs[-2], refs[-1]
        inv = lax.rsqrt(sq_ref[:, :1] / width + EPS_NORM)
        h = h_ref[...]
        ho_ref[...] = h.astype(BF16)
        n_ref[...] = (h * inv * g_ref[...]).astype(BF16)

    b0 = row0 // tr
    in_specs = [
        pl.BlockSpec((tr, cols), lambda i: (i, 0)),
        pl.BlockSpec((tr, 128), lambda i: (i, 0)),
        pl.BlockSpec((1, cols), lambda i: (0, 0)),
    ] + [ANY] * len(state)
    out = jax.ShapeDtypeStruct((total_rows, cols), BF16)
    return pl.pallas_call(
        body,
        grid=(rows // tr,),
        in_specs=in_specs,
        out_specs=[pl.BlockSpec((tr, cols), lambda i: (b0 + i, 0))] * 2,
        out_shape=[out, out],
        input_output_aliases={3 + i: i for i in range(len(state))},
        compiler_params=PARAMS,
        cost_estimate=pl.CostEstimate(flops=4 * rows * cols, bytes_accessed=8 * rows * cols, transcendentals=0),
    )(h, sq, gain, *state)


def solution(mesh):
    tp = mesh.shape["tp"]
    col_groups = mesh.shape["tp2"]

    def send(x, flip):
        return lax.ppermute(x, "tp", [(i, i ^ flip) for i in range(tp)])

    def inner(attn, w, res, gain):
        me = lax.axis_index("tp")
        rows_total, cols = res.shape
        pieces = {}
        dep = []
        near = None

        for t, (row, tm, col0, ncols, tn, splits) in enumerate(PLAN):
            if t == NEAR_AT:
                reps = rows_total // NEAR_ROWS
                other, own = products(attn, w, [(me ^ 1) * reps, me * reps], reps, NEAR_ROWS, 0, cols, 1024, (NEAR_ROWS,), dep)
                dep = [own]
                near = [own, send(other, 1)]
            per = rows_total // tm
            outs = products(attn, w, [(me ^ 2) * per + row // tm, (me ^ 3) * per + row // tm], 1, tm, col0, ncols, tn, splits, dep)
            dep = [outs[0]]
            for s, size in enumerate(splits):
                got = pieces.setdefault((row, size), ([], []))
                for b, flip in enumerate((2, 3)):
                    got[b].append(send(outs[b * len(splits) + s], flip))
                row += size

        gain2 = gain.reshape(1, cols)
        state = []
        for c, (row, size) in enumerate(sorted(pieces)):
            tr = min(size, 32)
            h, sq = add_rows(res, near, pieces[row, size], row, size, tr, col_groups, state[:1] if state else dep, c)
            state = norm_rows(h, sq, gain2, cols * col_groups, rows_total, row, tr, state)
        return tuple(state)

    row_spec = P(("dp", "tp"), "tp2")
    fn = jax.shard_map(inner, mesh=mesh, in_specs=(P("dp", "tp"), P("tp", "tp2"), row_spec, P("tp2")), out_specs=(row_spec, row_spec), check_vma=False)
    shapes = [jax.ShapeDtypeStruct(s, d) for s, d in (((4096, 16384), BF16), ((16384, 16384), BF16), ((4096, 16384), BF16), ((16384,), F32))]
    jax.eval_shape(fn, *shapes)
    return fn
```

time: 1000 us -> 1010 us (1.010)
  Pallas kernels: 414 us -> 474 us
  blocking collectives: 27.4 us -> 0 us
  waiting for transfers between devices: 534 us -> 513 us
    pallas_call x8 -> x14, Pallas kernels: 80.6 us -> 123 us  [the longest x7 84.1 us: add_rows(): pl.pallas_call(body, grid=(steps,), in_specs=in_specs, out_specs=[pl.Bloc...]
    psum x2 -> x0, blocking collectives: 27.4 us -> none  [the longest x1 19.4 us: inner(): sq_a = lax.psum(sq, 'tp2')]
    ppermute x17 -> x21, waiting for transfers between devices: 534 us -> 513 us  [send(): return lax.ppermute(x, 'tp', [(i, i ^ flip) for i in range(tp)])]
    pallas_call x7 -> x9, Pallas kernels: 333 us -> 351 us  [products(): pl.pallas_call(body, grid_spec=pltpu.PrefetchScalarGridSpec(num_scalar_pr...]
  transfers between devices with their start and end apart: 17 -> 21, of which waited for: 9 -> 11; matrix products, arithmetic and copies ran while one was open for 0% -> 0% of each run, Pallas kernels for 16% -> 20%
where the time goes in v2:
time: 1010 us
  waiting for transfers between devices  513 us (51%)
  Pallas kernels  474 us (47%)
  starting transfers between devices  19.8 us (2%)
    ppermute x21, waiting for transfers between devices, send(): return lax.ppermute(x, 'tp', [(i, i ^ flip) for i in range(tp)])  513 us
    pallas_call x9, Pallas kernels, products(): pl.pallas_call(body, grid_spec=pltpu.PrefetchScalarGridSpec(num_scalar_pr...  351 us
    pallas_call x7, Pallas kernels, add_rows(): pl.pallas_call(body, grid=(steps,), in_specs=in_specs, out_specs=[pl.Bloc...  84.1 us
    pallas_call x7, Pallas kernels, norm_rows(): pl.pallas_call(body, grid=(rows // tr,), in_specs=in_specs, out_specs=[pl...  39.1 us
  transfers between devices with their start and end apart: 21, of which 11 were waited for; matrix products, arithmetic and copies ran while one was open for 0% of the time, Pallas kernels for 20%

profile of v2, /device:TPU:0, one launch (start us, length us, event | category | flops | bytes accessed | tf_op | source)
XLA Modules:
  0.0 1008.0 jit_solution(14590212539762037121)
XLA Ops:
  0.6 4.4 shard_map.59
  5.0 6.9 shard_map.60
  11.9 12.0 %shard_map.61 = (bf16[128,2560]{1,0:T(8,128)(2,1)}, bf16[128,2560]{1,0:T(8,128)(2,1)}) custom-call(s32[1]{0:T(128)} %bitcast.6.refs_0_, s32[1]{0:T(128)} %bitcast.7.refs_1_, bf16[4096,4096]{1,0:T(8,128)(2,1)} %refs_3_.17, bf16[4096,4096]{1,0:T(8,128)(2,1)} %refs_3_.17, bf16[4096,8192]{1,0:T(8,128)(2,1)} %refs_4_.17, bf16[128,1024]{1,0:T(8,128)(2,1)} %get-tuple-element.51.refs_5_), custom_call_target="tpu_custom_call" | custom-call | flops 5368709120 | bytes 24379392 | tf_op jit(solution)/shard_map/pallas_call | solution.py:48
  23.9 17.3 %shard_map.62 = (bf16[128,4096]{1,0:T(8,128)(2,1)}, bf16[128,4096]{1,0:T(8,128)(2,1)}) custom-call(s32[1]{0:T(128)} %bitcast.6.refs_0_, s32[1]{0:T(128)} %bitcast.7.refs_1_, bf16[4096,4096]{1,0:T(8,128)(2,1)} %refs_3_.17, bf16[4096,4096]{1,0:T(8,128)(2,1)} %refs_3_.17, bf16[4096,8192]{1,0:T(8,128)(2,1)} %refs_4_.17, bf16[128,2560]{1,0:T(8,128)(2,1)} %get-tuple-element.52.refs_5_), custom_call_target="tpu_custom_call" | custom-call | flops 8589934592 | bytes 37748736 | tf_op jit(solution)/shard_map/pallas_call | solution.py:48
  41.2 32.0 %shard_map.63 = (bf16[128,8192]{1,0:T(8,128)(2,1)}, bf16[128,8192]{1,0:T(8,128)(2,1)}) custom-call(s32[1]{0:T(128)} %bitcast.4.refs_0_, s32[1]{0:T(128)} %bitcast.5.refs_1_, bf16[4096,4096]{1,0:T(8,128)(2,1)} %refs_3_.17, bf16[4096,4096]{1,0:T(8,128)(2,1)} %refs_3_.17, bf16[4096,8192]{1,0:T(8,128)(2,1)} %refs_4_.17, bf16[128,4096]{1,0:T(8,128)(2,1)} %get-tuple-element.53.refs_5_), custom_call_target="tpu_custom_call" | custom-call | flops 17179869184 | bytes 73400320 | tf_op jit(solution)/shard_map/pallas_call | solution.py:48
  73.3 41.9 %shard_map.64 = (bf16[256,8192]{1,0:T(8,128)(2,1)}, bf16[256,8192]{1,0:T(8,128)(2,1)}) custom-call(s32[1]{0:T(128)} %bitcast.2.refs_0_, s32[1]{0:T(128)} %bitcast.3.refs_1_, bf16[4096,4096]{1,0:T(8,128)(2,1)} %refs_3_.17, bf16[4096,4096]{1,0:T(8,128)(2,1)} %refs_3_.17, bf16[4096,8192]{1,0:T(8,128)(2,1)} %refs_4_.17, bf16[128,8192]{1,0:T(8,128)(2,1)} %get-tuple-element.54.refs_5_), custom_call_target="tpu_custom_call" | custom-call | flops 34359738368 | bytes 79691776 | tf_op jit(solution)/shard_map/pallas_call | solution.py:48
  115.2 152.5 %shard_map.65 = (bf16[1024,8192]{1,0:T(8,128)(2,1)}, bf16[1024,8192]{1,0:T(8,128)(2,1)}) custom-call(s32[1]{0:T(128)} %bitcast.refs_0_, s32[1]{0:T(128)} %bitcast.1.refs_1_, bf16[4096,4096]{1,0:T(8,128)(2,1)} %refs_3_.17, bf16[4096,4096]{1,0:T(8,128)(2,1)} %refs_3_.17, bf16[4096,8192]{1,0:T(8,128)(2,1)} %refs_4_.17, bf16[256,8192]{1,0:T(8,128)(2,1)} %get-tuple-element.55.refs_5_), custom_call_target="tpu_custom_call" | custom-call | flops 137438953472 | bytes 117440512 | tf_op jit(solution)/shard_map/pallas_call | solution.py:48
  267.7 0.8 collective-permute-start
  268.6 2.6 collective-permute-start.17
  271.2 2.0 collective-permute-start.14
  273.2 2.2 collective-permute-done.17.refs_7_
  275.4 1.9 collective-permute-start.18
  277.3 1.2 collective-permute-done.13.refs_3_
  278.5 0.5 collective-permute-start.19
  279.0 41.9 %shard_map.66 = (bf16[256,8192]{1,0:T(8,128)(2,1)}, bf16[256,8192]{1,0:T(8,128)(2,1)}) custom-call(s32[1]{0:T(128)} %bitcast.10.refs_0_, s32[1]{0:T(128)} %bitcast.11.refs_1_, bf16[4096,4096]{1,0:T(8,128)(2,1)} %refs_3_.17, bf16[4096,4096]{1,0:T(8,128)(2,1)} %refs_3_.17, bf16[4096,8192]{1,0:T(8,128)(2,1)} %refs_4_.17, ...), custom_call_target="tpu_custom_call" | custom-call | flops 34359738368 | bytes 79691776 | tf_op jit(solution)/shard_map/pallas_call | solution.py:48
  320.9 1.7 collective-permute-start.16
  323.0 1.1 collective-permute-start.20
  324.1 0.6 collective-permute-start.12
  324.7 41.9 %shard_map.67 = (bf16[128,8192]{1,0:T(8,128)(2,1)}, bf16[96,8192]{1,0:T(8,128)(2,1)}, bf16[32,8192]{1,0:T(8,128)(2,1)}, bf16[128,8192]{1,0:T(8,128)(2,1)}, bf16[...) custom-call(s32[1]{0:T(128)} %bitcast.8.refs_0_, s32[1]{0:T(128)} %bitcast.9.refs_1_, bf16[4096,4096]{1,0:T(8,128)(2,1)} %refs_3_.17, ...), custom_call_target="tpu_custom_call" | custom-call | flops 34359738368 | bytes 79691776 | tf_op jit(solution)/shard_map/pallas_call | solution.py:48
  366.6 48.9 %collective-permute-done.20.refs_10_ = bf16[128,4096]{1,0:T(8,128)(2,1)} collective-permute-done((bf16[128,4096]{1,0:T(8,128)(2,1)}, bf16[128,4096]{1,0:T(8,128)(2,1)}, u32[]{:S(2)}, u32[]{:S(2)}) %collective-permute-start.20) | collective-permute-done | bytes 1048608 | tf_op jit(solution)/shard_map/ppermute | solution.py:162
  415.5 0.6 collective-permute-start.6
  416.1 1.1 collective-permute-start.10
  417.3 43.2 %collective-permute-done.12.refs_4_ = bf16[128,8192]{1,0:T(8,128)(2,1)} collective-permute-done((bf16[128,8192]{1,0:T(8,128)(2,1)}, bf16[128,8192]{1,0:T(8,128)(2,1)}, u32[]{:S(2)}, u32[]{:S(2)}) %collective-permute-start.12) | collective-permute-done | bytes 2097184 | tf_op jit(solution)/shard_map/ppermute | solution.py:162
  460.4 0.6 collective-permute-start.8
  461.0 44.3 %collective-permute-done.6.refs_4_ = bf16[128,8192]{1,0:T(8,128)(2,1)} collective-permute-done((bf16[128,8192]{1,0:T(8,128)(2,1)}, bf16[128,8192]{1,0:T(8,128)(2,1)}, u32[]{:S(2)}, u32[]{:S(2)}) %collective-permute-start.6) | collective-permute-done | bytes 2097184 | tf_op jit(solution)/shard_map/ppermute | solution.py:162
  505.4 89.9 %collective-permute-done.10.refs_4_ = bf16[256,8192]{1,0:T(8,128)(2,1)} collective-permute-done((bf16[256,8192]{1,0:T(8,128)(2,1)}, bf16[256,8192]{1,0:T(8,128)(2,1)}, u32[]{:S(2)}, u32[]{:S(2)}) %collective-permute-start.10) | collective-permute-done | bytes 4194336 | tf_op jit(solution)/shard_map/ppermute | solution.py:162
  595.3 88.3 %collective-permute-done.9.refs_3_ = bf16[256,8192]{1,0:T(8,128)(2,1)} collective-permute-done((bf16[256,8192]{1,0:T(8,128)(2,1)}, bf16[256,8192]{1,0:T(8,128)(2,1)}, u32[]{:S(2)}, u32[]{:S(2)}) %collective-permute-start.9) | collective-permute-done | bytes 4194336 | tf_op jit(solution)/shard_map/ppermute | solution.py:162
  683.5 2.5 collective-permute-start.3
  686.0 89.0 %collective-permute-done.8.refs_4_ = bf16[256,8192]{1,0:T(8,128)(2,1)} collective-permute-done((bf16[256,8192]{1,0:T(8,128)(2,1)}, bf16[256,8192]{1,0:T(8,128)(2,1)}, u32[]{:S(2)}, u32[]{:S(2)}) %collective-permute-start.8) | collective-permute-done | bytes 4194336 | tf_op jit(solution)/shard_map/ppermute | solution.py:162
  775.3 88.0 %collective-permute-done.7.refs_3_ = bf16[256,8192]{1,0:T(8,128)(2,1)} collective-permute-done((bf16[256,8192]{1,0:T(8,128)(2,1)}, bf16[256,8192]{1,0:T(8,128)(2,1)}, u32[]{:S(2)}, u32[]{:S(2)}) %collective-permute-start.7) | collective-permute-done | bytes 4194336 | tf_op jit(solution)/shard_map/ppermute | solution.py:162
  863.3 2.5 collective-permute-start.1
  865.8 0.6 collective-permute-start.2
  866.4 10.9 %shard_map.68 = (f32[128,8192]{1,0:T(8,128)}, f32[128,128]{1,0:T(8,128)}) custom-call(bf16[1024,8192]{1,0:T(8,128)(2,1)} %refs_0_.13, bf16[1024,8192]{1,0:T(8,128)(2,1)} %get-tuple-element.56.refs_5_.refs_1_, bf16[1024,8192]{1,0:T(8,128)(2,1)} %collective-permute-done.refs_2_, bf16[128,512]{1,0:T(8,128)(2,1)} %collective-permute-done.13.refs_3_, ...), custom_call_target="tpu_custom_call" | custom-call | flops 8388608 | bytes 14680064 | tf_op jit(solution)/shard_map/pallas_call | solution.py:111
  877.3 4.8 shard_map.69
  882.1 10.1 %shard_map.70 = (f32[128,8192]{1,0:T(8,128)}, f32[128,128]{1,0:T(8,128)}) custom-call(bf16[1024,8192]{1,0:T(8,128)(2,1)} %refs_0_.13, bf16[1024,8192]{1,0:T(8,128)(2,1)} %get-tuple-element.56.refs_5_.refs_1_, bf16[1024,8192]{1,0:T(8,128)(2,1)} %collective-permute-done.refs_2_, bf16[128,8192]{1,0:T(8,128)(2,1)} %collective-permute-done.11.refs_3_, ...), custom_call_target="tpu_custom_call" | custom-call | flops 8388608 | bytes 14680064 | tf_op jit(solution)/shard_map/pallas_call | solution.py:111
  892.2 4.8 shard_map.71
  897.0 18.1 %shard_map.72 = (f32[256,8192]{1,0:T(8,128)}, f32[256,128]{1,0:T(8,128)}) custom-call(bf16[1024,8192]{1,0:T(8,128)(2,1)} %refs_0_.13, bf16[1024,8192]{1,0:T(8,128)(2,1)} %get-tuple-element.56.refs_5_.refs_1_, bf16[1024,8192]{1,0:T(8,128)(2,1)} %collective-permute-done.refs_2_, bf16[256,8192]{1,0:T(8,128)(2,1)} %collective-permute-done.9.refs_3_, ...), custom_call_target="tpu_custom_call" | custom-call | flops 16777216 | bytes 29360128 | tf_op jit(solution)/shard_map/pallas_call | solution.py:111
  915.1 9.0 shard_map.73
  924.1 17.1 %shard_map.74 = (f32[256,8192]{1,0:T(8,128)}, f32[256,128]{1,0:T(8,128)}) custom-call(bf16[1024,8192]{1,0:T(8,128)(2,1)} %refs_0_.13, bf16[1024,8192]{1,0:T(8,128)(2,1)} %get-tuple-element.56.refs_5_.refs_1_, bf16[1024,8192]{1,0:T(8,128)(2,1)} %collective-permute-done.refs_2_, bf16[256,8192]{1,0:T(8,128)(2,1)} %collective-permute-done.7.refs_3_, ...), custom_call_target="tpu_custom_call" | custom-call | flops 16777216 | bytes 29360128 | tf_op jit(solution)/shard_map/pallas_call | solution.py:111
  941.2 9.0 shard_map.75
  950.2 11.1 %shard_map.76 = (f32[128,8192]{1,0:T(8,128)}, f32[128,128]{1,0:T(8,128)}) custom-call(bf16[1024,8192]{1,0:T(8,128)(2,1)} %refs_0_.13, bf16[1024,8192]{1,0:T(8,128)(2,1)} %get-tuple-element.56.refs_5_.refs_1_, bf16[1024,8192]{1,0:T(8,128)(2,1)} %collective-permute-done.refs_2_, bf16[128,8192]{1,0:T(8,128)(2,1)} %collective-permute-done.5.refs_3_, ...), custom_call_target="tpu_custom_call" | custom-call | flops 8388608 | bytes 14680064 | tf_op jit(solution)/shard_map/pallas_call | solution.py:111
  961.3 4.8 shard_map.77
  966.1 11.2 %collective-permute-done.4.refs_4_ = bf16[96,8192]{1,0:T(8,128)(2,1)} collective-permute-done((bf16[96,8192]{1,0:T(8,128)(2,1)}, bf16[96,8192]{1,0:T(8,128)(2,1)}, u32[]{:S(2)}, u32[]{:S(2)}) %collective-permute-start.4) | collective-permute-done | bytes 1572896 | tf_op jit(solution)/shard_map/ppermute | solution.py:162
  977.3 10.0 shard_map.78
  987.3 4.4 shard_map.79
  991.7 7.2 collective-permute-done.2.refs_4_
  998.9 6.7 shard_map.80
  1005.7 2.3 shard_map.81
  (17 shorter events, 0.7 us)
Async XLA Ops:
  267.7 598.1 %collective-permute-start = (bf16[1024,8192]{1,0:T(8,128)(2,1)}, bf16[1024,8192]{1,0:T(8,128)(2,1)}, u32[]{:S(2)}, u32[]{:S(2)}) collective-permute-start(bf16[1024,8192]{1,0:T(8,128)(2,1)} %get-tuple-element.57), channel_id=1, source_target_pairs={{0,1},{1,0},{2,3},{3,2},{4,5},{5,4},{6,7},{7,6}} | collective-permute-start | bytes 50331656 | tf_op jit(solution)/shard_map/ppermute | solution.py:162
  268.6 6.8 collective-permute-start.17
  271.2 7.4 collective-permute-start.13
  271.2 51.5 %collective-permute-start.14 = (bf16[128,1024]{1,0:T(8,128)(2,1)}, bf16[128,1024]{1,0:T(8,128)(2,1)}, u32[]{:S(2)}, u32[]{:S(2)}) collective-permute-start(bf16[128,1024]{1,0:T(8,128)(2,1)} %get-tuple-element.51.refs_5_), channel_id=1, source_target_pairs={{0,2},{1,3},{2,0},{3,1},{4,6},{5,7},{6,4},{7,5}} | collective-permute-start | bytes 786440 | tf_op jit(solution)/shard_map/ppermute | solution.py:162
  273.2 50.9 %collective-permute-start.15 = (bf16[128,2560]{1,0:T(8,128)(2,1)}, bf16[128,2560]{1,0:T(8,128)(2,1)}, u32[]{:S(2)}, u32[]{:S(2)}) collective-permute-start(bf16[128,2560]{1,0:T(8,128)(2,1)} %get-tuple-element.52.refs_5_), channel_id=1, source_target_pairs={{0,2},{1,3},{2,0},{3,1},{4,6},{5,7},{6,4},{7,5}} | collective-permute-start | bytes 1966088 | tf_op jit(solution)/shard_map/ppermute | solution.py:162
  275.4 45.6 %collective-permute-start.18 = (bf16[128,1024]{1,0:T(8,128)(2,1)}, bf16[128,1024]{1,0:T(8,128)(2,1)}, u32[]{:S(2)}, u32[]{:S(2)}) collective-permute-start(bf16[128,1024]{1,0:T(8,128)(2,1)} %get-tuple-element.69), channel_id=1, source_target_pairs={{0,3},{1,2},{2,1},{3,0},{4,7},{5,6},{6,5},{7,4}} | collective-permute-start | bytes 786440 | tf_op jit(solution)/shard_map/ppermute | solution.py:162
  278.5 44.5 %collective-permute-start.19 = (bf16[128,2560]{1,0:T(8,128)(2,1)}, bf16[128,2560]{1,0:T(8,128)(2,1)}, u32[]{:S(2)}, u32[]{:S(2)}) collective-permute-start(bf16[128,2560]{1,0:T(8,128)(2,1)} %get-tuple-element.70), channel_id=1, source_target_pairs={{0,3},{1,2},{2,1},{3,0},{4,7},{5,6},{6,5},{7,4}} | collective-permute-start | bytes 1966088 | tf_op jit(solution)/shard_map/ppermute | solution.py:162
  320.9 95.2 %collective-permute-start.16 = (bf16[128,4096]{1,0:T(8,128)(2,1)}, bf16[128,4096]{1,0:T(8,128)(2,1)}, u32[]{:S(2)}, u32[]{:S(2)}) collective-permute-start(bf16[128,4096]{1,0:T(8,128)(2,1)} %get-tuple-element.53.refs_5_), channel_id=1, source_target_pairs={{0,2},{1,3},{2,0},{3,1},{4,6},{5,7},{6,4},{7,5}} | collective-permute-start | bytes 3145736 | tf_op jit(solution)/shard_map/ppermute | solution.py:162
  322.6 137.8 %collective-permute-start.11 = (bf16[128,8192]{1,0:T(8,128)(2,1)}, bf16[128,8192]{1,0:T(8,128)(2,1)}, u32[]{:S(2)}, u32[]{:S(2)}) collective-permute-start(bf16[128,8192]{1,0:T(8,128)(2,1)} %get-tuple-element.54.refs_5_), channel_id=1, source_target_pairs={{0,2},{1,3},{2,0},{3,1},{4,6},{5,7},{6,4},{7,5}} | collective-permute-start | bytes 6291464 | tf_op jit(solution)/shard_map/ppermute | solution.py:162
  323.0 92.5 %collective-permute-start.20 = (bf16[128,4096]{1,0:T(8,128)(2,1)}, bf16[128,4096]{1,0:T(8,128)(2,1)}, u32[]{:S(2)}, u32[]{:S(2)}) collective-permute-start(bf16[128,4096]{1,0:T(8,128)(2,1)} %get-tuple-element.71), channel_id=1, source_target_pairs={{0,3},{1,2},{2,1},{3,0},{4,7},{5,6},{6,5},{7,4}} | collective-permute-start | bytes 3145736 | tf_op jit(solution)/shard_map/ppermute | solution.py:162
  324.1 136.3 %collective-permute-start.12 = (bf16[128,8192]{1,0:T(8,128)(2,1)}, bf16[128,8192]{1,0:T(8,128)(2,1)}, u32[]{:S(2)}, u32[]{:S(2)}) collective-permute-start(bf16[128,8192]{1,0:T(8,128)(2,1)} %get-tuple-element.67), channel_id=1, source_target_pairs={{0,3},{1,2},{2,1},{3,0},{4,7},{5,6},{6,5},{7,4}} | collective-permute-start | bytes 6291464 | tf_op jit(solution)/shard_map/ppermute | solution.py:162
  415.5 89.9 %collective-permute-start.6 = (bf16[128,8192]{1,0:T(8,128)(2,1)}, bf16[128,8192]{1,0:T(8,128)(2,1)}, u32[]{:S(2)}, u32[]{:S(2)}) collective-permute-start(bf16[128,8192]{1,0:T(8,128)(2,1)} %get-tuple-element.64), channel_id=1, source_target_pairs={{0,3},{1,2},{2,1},{3,0},{4,7},{5,6},{6,5},{7,4}} | collective-permute-start | bytes 6291464 | tf_op jit(solution)/shard_map/ppermute | solution.py:162
  416.1 179.2 %collective-permute-start.10 = (bf16[256,8192]{1,0:T(8,128)(2,1)}, bf16[256,8192]{1,0:T(8,128)(2,1)}, u32[]{:S(2)}, u32[]{:S(2)}) collective-permute-start(bf16[256,8192]{1,0:T(8,128)(2,1)} %get-tuple-element.66), channel_id=1, source_target_pairs={{0,3},{1,2},{2,1},{3,0},{4,7},{5,6},{6,5},{7,4}} | collective-permute-start | bytes 12582920 | tf_op jit(solution)/shard_map/ppermute | solution.py:162
  460.4 223.1 %collective-permute-start.9 = (bf16[256,8192]{1,0:T(8,128)(2,1)}, bf16[256,8192]{1,0:T(8,128)(2,1)}, u32[]{:S(2)}, u32[]{:S(2)}) collective-permute-start(bf16[256,8192]{1,0:T(8,128)(2,1)} %get-tuple-element.55.refs_5_), channel_id=1, source_target_pairs={{0,2},{1,3},{2,0},{3,1},{4,6},{5,7},{6,4},{7,5}} | collective-permute-start | bytes 12582920 | tf_op jit(solution)/shard_map/ppermute | solution.py:162
  460.4 314.6 %collective-permute-start.8 = (bf16[256,8192]{1,0:T(8,128)(2,1)}, bf16[256,8192]{1,0:T(8,128)(2,1)}, u32[]{:S(2)}, u32[]{:S(2)}) collective-permute-start(bf16[256,8192]{1,0:T(8,128)(2,1)} %get-tuple-element.65), channel_id=1, source_target_pairs={{0,3},{1,2},{2,1},{3,0},{4,7},{5,6},{6,5},{7,4}} | collective-permute-start | bytes 12582920 | tf_op jit(solution)/shard_map/ppermute | solution.py:162
  505.4 357.9 %collective-permute-start.7 = (bf16[256,8192]{1,0:T(8,128)(2,1)}, bf16[256,8192]{1,0:T(8,128)(2,1)}, u32[]{:S(2)}, u32[]{:S(2)}) collective-permute-start(bf16[256,8192]{1,0:T(8,128)(2,1)} %get-tuple-element.58.refs_5_), channel_id=1, source_target_pairs={{0,2},{1,3},{2,0},{3,1},{4,6},{5,7},{6,4},{7,5}} | collective-permute-start | bytes 12582920 | tf_op jit(solution)/shard_map/ppermute | solution.py:162
  595.3 354.9 %collective-permute-start.5 = (bf16[128,8192]{1,0:T(8,128)(2,1)}, bf16[128,8192]{1,0:T(8,128)(2,1)}, u32[]{:S(2)}, u32[]{:S(2)}) collective-permute-start(bf16[128,8192]{1,0:T(8,128)(2,1)} %get-tuple-element.63.refs_11_), channel_id=1, source_target_pairs={{0,2},{1,3},{2,0},{3,1},{4,6},{5,7},{6,4},{7,5}} | collective-permute-start | bytes 6291464 | tf_op jit(solution)/shard_map/ppermute | solution.py:162
  683.5 282.6 %collective-permute-start.3 = (bf16[96,8192]{1,0:T(8,128)(2,1)}, bf16[96,8192]{1,0:T(8,128)(2,1)}, u32[]{:S(2)}, u32[]{:S(2)}) collective-permute-start(bf16[96,8192]{1,0:T(8,128)(2,1)} %get-tuple-element.61), channel_id=1, source_target_pairs={{0,2},{1,3},{2,0},{3,1},{4,6},{5,7},{6,4},{7,5}} | collective-permute-start | bytes 4718600 | tf_op jit(solution)/shard_map/ppermute | solution.py:162
  775.0 202.2 %collective-permute-start.4 = (bf16[96,8192]{1,0:T(8,128)(2,1)}, bf16[96,8192]{1,0:T(8,128)(2,1)}, u32[]{:S(2)}, u32[]{:S(2)}) collective-permute-start(bf16[96,8192]{1,0:T(8,128)(2,1)} %get-tuple-element.62), channel_id=1, source_target_pairs={{0,3},{1,2},{2,1},{3,0},{4,7},{5,6},{6,5},{7,4}} | collective-permute-start | bytes 4718600 | tf_op jit(solution)/shard_map/ppermute | solution.py:162
  863.3 128.4 %collective-permute-start.1 = (bf16[32,8192]{1,0:T(8,128)(2,1)}, bf16[32,8192]{1,0:T(8,128)(2,1)}, u32[]{:S(2)}, u32[]{:S(2)}) collective-permute-start(bf16[32,8192]{1,0:T(8,128)(2,1)} %get-tuple-element.59), channel_id=1, source_target_pairs={{0,2},{1,3},{2,0},{3,1},{4,6},{5,7},{6,4},{7,5}} | collective-permute-start | bytes 1572872 | tf_op jit(solution)/shard_map/ppermute | solution.py:162
  865.8 133.1 %collective-permute-start.2 = (bf16[32,8192]{1,0:T(8,128)(2,1)}, bf16[32,8192]{1,0:T(8,128)(2,1)}, u32[]{:S(2)}, u32[]{:S(2)}) collective-permute-start(bf16[32,8192]{1,0:T(8,128)(2,1)} %get-tuple-element.60), channel_id=1, source_target_pairs={{0,3},{1,2},{2,1},{3,0},{4,7},{5,6},{6,5},{7,4}} | collective-permute-start | bytes 1572872 | tf_op jit(solution)/shard_map/ppermute | solution.py:162

commit v3 on v2

--- a/solution.py
+++ b/solution.py
@@ -12,16 +12,18 @@
 
 ANY = pl.BlockSpec(memory_space=pl.ANY)
 PARAMS = pltpu.CompilerParams(vmem_limit_bytes=VMEM_BYTES)
-
+SMALL_VMEM = 50 * 2**20
+
+BOTH = (2, 3)
 PLAN = (
-    (0, 128, 0, 512, 256, (128,)),
-    (0, 128, 512, 1024, 256, (128,)),
-    (0, 128, 1536, 2560, 512, (128,)),
-    (0, 128, 4096, 4096, 512, (128,)),
-    (128, 128, 0, 8192, 512, (128,)),
-    (256, 256, 0, 8192, 512, (256,)),
-    (512, 256, 0, 8192, 512, (256,)),
-    (768, 256, 0, 8192, 512, (128, 96, 32)),
+    ((2,), 0, 256, 0, 1024, 256, (256,)),
+    ((3,), 0, 256, 0, 1024, 256, (256,)),
+    (BOTH, 0, 256, 1024, 1536, 512, (256,)),
+    (BOTH, 0, 256, 2560, 2560, 512, (256,)),
+    (BOTH, 0, 256, 5120, 3072, 512, (256,)),
+    (BOTH, 256, 256, 0, 8192, 512, (256,)),
+    (BOTH, 512, 256, 0, 8192, 512, (256,)),
+    (BOTH, 768, 256, 0, 8192, 512, (128, 80, 32, 16)),
 )
 NEAR_AT = 6
 NEAR_ROWS = 256
@@ -84,11 +86,10 @@
         base = 0
         for c, width in enumerate(widths):
             sl = slice(base, base + width)
-            y = near_refs[0][:, sl].astype(F32)
-            for ref in near_refs[1:]:
-                y = y + ref[:, sl].astype(F32)
-            for g in range(nf):
-                y = y + far_refs[g * per + c][...].astype(F32)
+            terms = [ref[:, sl] for ref in near_refs] + [far_refs[g * per + c][...] for g in range(nf)]
+            y = terms[0].astype(F32)
+            for term in terms[1:]:
+                y = y + term.astype(F32)
             h = r_ref[:, sl].astype(F32) + y
             h_ref[:, sl] = h
             total = total + jnp.sum(h * h, axis=-1, keepdims=True)
@@ -105,7 +106,7 @@
             copy.wait()
             sq_ref[...] = mine[...] + theirs[...]
 
-    b0 = row0 // tr
+    b0 = row0 // tr if near else 0
     full = pl.BlockSpec((tr, cols), lambda i: (b0 + i, 0))
     in_specs = [full] * (1 + nn) + [pl.BlockSpec((tr, piece.shape[1]), lambda i: (i, 0)) for piece in flat] + [ANY] * len(deps)
     return pl.pallas_call(
@@ -120,9 +121,29 @@
             pltpu.SemaphoreType.DMA,
             pltpu.SemaphoreType.DMA,
         ],
-        compiler_params=pltpu.CompilerParams(vmem_limit_bytes=VMEM_BYTES, collective_id=collective_id, has_side_effects=True),
+        compiler_params=pltpu.CompilerParams(vmem_limit_bytes=SMALL_VMEM, collective_id=collective_id, has_side_effects=True),
         cost_estimate=pl.CostEstimate(flops=8 * rows * cols, bytes_accessed=14 * rows * cols, transcendentals=0),
     )(res, *near, *flat, *deps)
+
+
+def near_sum(res, near, row0, rows, deps):
+    cols = res.shape[1]
+
+    def body(*refs):
+        total = refs[0][...].astype(F32)
+        for ref in refs[1:1 + len(near)]:
+            total = total + ref[...].astype(F32)
+        refs[-1][...] = total
+
+    return pl.pallas_call(
+        body,
+        grid=(1,),
+        in_specs=[pl.BlockSpec((rows, cols), lambda i: (row0 // rows, 0))] * (1 + len(near)) + [ANY] * len(deps),
+        out_specs=pl.BlockSpec((rows, cols), lambda i: (0, 0)),
+        out_shape=jax.ShapeDtypeStruct((rows, cols), F32),
+        compiler_params=pltpu.CompilerParams(vmem_limit_bytes=SMALL_VMEM),
+        cost_estimate=pl.CostEstimate(flops=2 * rows * cols, bytes_accessed=10 * rows * cols, transcendentals=0),
+    )(res, *near, *deps)
 
 
 def norm_rows(h, sq, gain, width, total_rows, row0, tr, state):
@@ -149,7 +170,7 @@
         out_specs=[pl.BlockSpec((tr, cols), lambda i: (b0 + i, 0))] * 2,
         out_shape=[out, out],
         input_output_aliases={3 + i: i for i in range(len(state))},
-        compiler_params=PARAMS,
+        compiler_params=pltpu.CompilerParams(vmem_limit_bytes=SMALL_VMEM),
         cost_estimate=pl.CostEstimate(flops=4 * rows * cols, bytes_accessed=8 * rows * cols, transcendentals=0),
     )(h, sq, gain, *state)
 
@@ -168,26 +189,30 @@
         dep = []
         near = None
 
-        for t, (row, tm, col0, ncols, tn, splits) in enumerate(PLAN):
+        for t, (flips, row, tm, col0, ncols, tn, splits) in enumerate(PLAN):
             if t == NEAR_AT:
                 reps = rows_total // NEAR_ROWS
                 other, own = products(attn, w, [(me ^ 1) * reps, me * reps], reps, NEAR_ROWS, 0, cols, 1024, (NEAR_ROWS,), dep)
                 dep = [own]
                 near = [own, send(other, 1)]
             per = rows_total // tm
-            outs = products(attn, w, [(me ^ 2) * per + row // tm, (me ^ 3) * per + row // tm], 1, tm, col0, ncols, tn, splits, dep)
+            outs = products(attn, w, [(me ^ flip) * per + row // tm for flip in flips], 1, tm, col0, ncols, tn, splits, dep)
             dep = [outs[0]]
             for s, size in enumerate(splits):
                 got = pieces.setdefault((row, size), ([], []))
-                for b, flip in enumerate((2, 3)):
-                    got[b].append(send(outs[b * len(splits) + s], flip))
+                for b, flip in enumerate(flips):
+                    got[BOTH.index(flip)].append(send(outs[b * len(splits) + s], flip))
                 row += size
 
         gain2 = gain.reshape(1, cols)
         state = []
-        for c, (row, size) in enumerate(sorted(pieces)):
-            tr = min(size, 32)
-            h, sq = add_rows(res, near, pieces[row, size], row, size, tr, col_groups, state[:1] if state else dep, c)
+        chunks = sorted(pieces)
+        for c, (row, size) in enumerate(chunks):
+            tr = 32 if (row | size) % 32 == 0 else 16
+            if c == 1:
+                ready = near_sum(res, near, *chunks[-1], state[:1])
+            terms = (res, near) if c < len(chunks) - 1 else (ready, [])
+            h, sq = add_rows(*terms, pieces[row, size], row, size, tr, col_groups, state[:1] if state else dep, c)
             state = norm_rows(h, sq, gain2, cols * col_groups, rows_total, row, tr, state)
         return tuple(state)
 

time: 1010 us -> 1050 us (1.040)
  waiting for transfers between devices: 513 us -> 554 us
  Pallas kernels: 474 us -> 459 us
    ppermute x21, waiting for transfers between devices: 513 us -> 554 us  [send(): return lax.ppermute(x, 'tp', [(i, i ^ flip) for i in range(tp)])]
    pallas_call x9, Pallas kernels: 351 us -> 338 us  [products(): pl.pallas_call(body, grid_spec=pltpu.PrefetchScalarGridSpec(num_scalar_pr...]
  transfers between devices with their start and end apart: 21 -> 21, of which waited for: 11 -> 8; matrix products, arithmetic and copies ran while one was open for 0% -> 0% of each run, Pallas kernels for 20% -> 19%
where the time goes in v3:
time: 1050 us; the launch traced here: 1040 us
  waiting for transfers between devices  554 us (53%)
  Pallas kernels  459 us (44%)
  starting transfers between devices  25.8 us (2%)
    ppermute x21, waiting for transfers between devices, send(): return lax.ppermute(x, 'tp', [(i, i ^ flip) for i in range(tp)])  554 us
    pallas_call x9, Pallas kernels, products(): pl.pallas_call(body, grid_spec=pltpu.PrefetchScalarGridSpec(num_scalar_pr...  338 us
    pallas_call x7, Pallas kernels, add_rows(): pl.pallas_call(body, grid=(steps,), in_specs=in_specs, out_specs=[pl.Bloc...  84.1 us
    pallas_call x7, Pallas kernels, norm_rows(): pl.pallas_call(body, grid=(rows // tr,), in_specs=in_specs, out_specs=[pl...  36.2 us
    ppermute x21, starting transfers between devices, send(): return lax.ppermute(x, 'tp', [(i, i ^ flip) for i in range(tp)])  25.8 us
  transfers between devices with their start and end apart: 21, of which 8 were waited for; matrix products, arithmetic and copies ran while one was open for 0% of the time, Pallas kernels for 19%

profile of v3, /device:TPU:0, one launch (start us, length us, event | category | flops | bytes accessed | tf_op | source)
XLA Modules:
  0.0 1042.7 jit_solution(8392410122283719602)
XLA Ops:
  0.6 6.9 shard_map.59.refs_3_
  7.5 6.9 shard_map.60.refs_5_
  14.4 11.3 %shard_map.61 = (bf16[256,1536]{1,0:T(8,128)(2,1)}, bf16[256,1536]{1,0:T(8,128)(2,1)}) custom-call(s32[1]{0:T(128)} %bitcast.4.refs_0_, s32[1]{0:T(128)} %bitcast.5.refs_0_.refs_1_, bf16[4096,4096]{1,0:T(8,128)(2,1)} %refs_3_.13, bf16[4096,4096]{1,0:T(8,128)(2,1)} %refs_3_.13, bf16[4096,8192]{1,0:T(8,128)(2,1)} %refs_4_.13, bf16[256,1024]{1,0:T(8,128)(2,1)} %shard_map.60.refs_5_), custom_call_target="tpu_custom_call" | custom-call | flops 6442450944 | bytes 18350080 | tf_op jit(solution)/shard_map/pallas_call | solution.py:50
  25.7 16.0 %shard_map.62 = (bf16[256,2560]{1,0:T(8,128)(2,1)}, bf16[256,2560]{1,0:T(8,128)(2,1)}) custom-call(s32[1]{0:T(128)} %bitcast.4.refs_0_, s32[1]{0:T(128)} %bitcast.5.refs_0_.refs_1_, bf16[4096,4096]{1,0:T(8,128)(2,1)} %refs_3_.13, bf16[4096,4096]{1,0:T(8,128)(2,1)} %refs_3_.13, bf16[4096,8192]{1,0:T(8,128)(2,1)} %refs_4_.13, ...), custom_call_target="tpu_custom_call" | custom-call | flops 10737418240 | bytes 27787264 | tf_op jit(solution)/shard_map/pallas_call | solution.py:50
  41.7 18.4 %shard_map.63 = (bf16[256,3072]{1,0:T(8,128)(2,1)}, bf16[256,3072]{1,0:T(8,128)(2,1)}) custom-call(s32[1]{0:T(128)} %bitcast.4.refs_0_, s32[1]{0:T(128)} %bitcast.5.refs_0_.refs_1_, bf16[4096,4096]{1,0:T(8,128)(2,1)} %refs_3_.13, bf16[4096,4096]{1,0:T(8,128)(2,1)} %refs_3_.13, bf16[4096,8192]{1,0:T(8,128)(2,1)} %refs_4_.13, ...), custom_call_target="tpu_custom_call" | custom-call | flops 12884901888 | bytes 32505856 | tf_op jit(solution)/shard_map/pallas_call | solution.py:50
  60.1 42.0 %shard_map.64 = (bf16[256,8192]{1,0:T(8,128)(2,1)}, bf16[256,8192]{1,0:T(8,128)(2,1)}) custom-call(s32[1]{0:T(128)} %bitcast.2.refs_0_, s32[1]{0:T(128)} %bitcast.3.refs_1_, bf16[4096,4096]{1,0:T(8,128)(2,1)} %refs_3_.13, bf16[4096,4096]{1,0:T(8,128)(2,1)} %refs_3_.13, bf16[4096,8192]{1,0:T(8,128)(2,1)} %refs_4_.13, bf16[256,3072]{1,0:T(8,128)(2,1)} %get-tuple-element.50.refs_5_), custom_call_target="tpu_custom_call" | custom-call | flops 34359738368 | bytes 79691776 | tf_op jit(solution)/shard_map/pallas_call | solution.py:50
  102.1 152.5 %shard_map.65 = (bf16[1024,8192]{1,0:T(8,128)(2,1)}, bf16[1024,8192]{1,0:T(8,128)(2,1)}) custom-call(s32[1]{0:T(128)} %bitcast.refs_0_, s32[1]{0:T(128)} %bitcast.1.refs_1_, bf16[4096,4096]{1,0:T(8,128)(2,1)} %refs_3_.13, bf16[4096,4096]{1,0:T(8,128)(2,1)} %refs_3_.13, bf16[4096,8192]{1,0:T(8,128)(2,1)} %refs_4_.13, bf16[256,8192]{1,0:T(8,128)(2,1)} %get-tuple-element.51.refs_5_), custom_call_target="tpu_custom_call" | custom-call | flops 137438953472 | bytes 117440512 | tf_op jit(solution)/shard_map/pallas_call | solution.py:50
  254.6 0.8 collective-permute-start
  255.4 2.6 collective-permute-start.5
  258.0 2.0 collective-permute-start.2
  260.1 42.0 %shard_map.66 = (bf16[256,8192]{1,0:T(8,128)(2,1)}, bf16[256,8192]{1,0:T(8,128)(2,1)}) custom-call(s32[1]{0:T(128)} %bitcast.8.refs_0_, s32[1]{0:T(128)} %bitcast.9.refs_1_, bf16[4096,4096]{1,0:T(8,128)(2,1)} %refs_3_.13, bf16[4096,4096]{1,0:T(8,128)(2,1)} %refs_3_.13, bf16[4096,8192]{1,0:T(8,128)(2,1)} %refs_4_.13, ...), custom_call_target="tpu_custom_call" | custom-call | flops 34359738368 | bytes 79691776 | tf_op jit(solution)/shard_map/pallas_call | solution.py:50
  302.0 0.8 collective-permute-start.6
  302.8 1.0 collective-permute-start.7
  303.8 42.0 %shard_map.67 = (bf16[128,8192]{1,0:T(8,128)(2,1)}, bf16[80,8192]{1,0:T(8,128)(2,1)}, bf16[32,8192]{1,0:T(8,128)(2,1)}, bf16[16,8192]{1,0:T(8,128)(2,1)}, bf16[1...) custom-call(s32[1]{0:T(128)} %bitcast.6.refs_0_, ...), custom_call_target="tpu_custom_call" | custom-call | flops 34359738368 | bytes 79691776 | tf_op jit(solution)/shard_map/pallas_call | solution.py:50
  345.8 2.0 collective-permute-start.13
  347.9 23.9 %collective-permute-done.7.refs_9_ = bf16[256,2560]{1,0:T(8,128)(2,1)} collective-permute-done((bf16[256,2560]{1,0:T(8,128)(2,1)}, bf16[256,2560]{1,0:T(8,128)(2,1)}, u32[]{:S(2)}, u32[]{:S(2)}) %collective-permute-start.7) | collective-permute-done | bytes 1310752 | tf_op jit(solution)/shard_map/ppermute | solution.py:183
  371.8 1.9 collective-permute-start.16
  373.7 26.4 %collective-permute-done.13.refs_3_ = bf16[80,8192]{1,0:T(8,128)(2,1)S(1)} collective-permute-done((bf16[80,8192]{1,0:T(8,128)(2,1)}, bf16[80,8192]{1,0:T(8,128)(2,1)S(1)}, u32[]{:S(2)}, u32[]{:S(2)}) %collective-permute-start.13) | collective-permute-done | bytes 1310752 | tf_op jit(solution)/shard_map/ppermute | solution.py:183
  400.1 2.1 collective-permute-start.4
  402.2 31.3 %collective-permute-done.8.refs_10_ = bf16[256,3072]{1,0:T(8,128)(2,1)S(1)} collective-permute-done((bf16[256,3072]{1,0:T(8,128)(2,1)}, bf16[256,3072]{1,0:T(8,128)(2,1)S(1)}, u32[]{:S(2)}, u32[]{:S(2)}) %collective-permute-start.8) | collective-permute-done | bytes 1572896 | tf_op jit(solution)/shard_map/ppermute | solution.py:183
  433.6 2.1 collective-permute-start.20
  435.7 121.7 %collective-permute-done.4.refs_6_ = bf16[256,3072]{1,0:T(8,128)(2,1)S(1)} collective-permute-done((bf16[256,3072]{1,0:T(8,128)(2,1)}, bf16[256,3072]{1,0:T(8,128)(2,1)S(1)}, u32[]{:S(2)}, u32[]{:S(2)}) %collective-permute-start.4) | collective-permute-done | bytes 1572896 | tf_op jit(solution)/shard_map/ppermute | solution.py:183
  557.4 2.1 collective-permute-start.19
  559.5 1.4 copy-done.6
  561.0 86.1 %collective-permute-done.20.refs_4_ = bf16[256,8192]{1,0:T(8,128)(2,1)S(1)} collective-permute-done((bf16[256,8192]{1,0:T(8,128)(2,1)}, bf16[256,8192]{1,0:T(8,128)(2,1)S(1)}, u32[]{:S(2)}, u32[]{:S(2)}) %collective-permute-start.20) | collective-permute-done | bytes 4194336 | tf_op jit(solution)/shard_map/ppermute | solution.py:183
  647.0 1.8 collective-permute-start.14
  648.8 88.3 %collective-permute-done.19.refs_3_ = bf16[256,8192]{1,0:T(8,128)(2,1)S(1)} collective-permute-done((bf16[256,8192]{1,0:T(8,128)(2,1)}, bf16[256,8192]{1,0:T(8,128)(2,1)S(1)}, u32[]{:S(2)}, u32[]{:S(2)}) %collective-permute-start.19) | collective-permute-done | bytes 4194336 | tf_op jit(solution)/shard_map/ppermute | solution.py:183
  737.2 2.1 collective-permute-start.11
  739.3 87.5 %collective-permute-done.18.refs_4_ = bf16[256,8192]{1,0:T(8,128)(2,1)S(1)} collective-permute-done((bf16[256,8192]{1,0:T(8,128)(2,1)}, bf16[256,8192]{1,0:T(8,128)(2,1)S(1)}, u32[]{:S(2)}, u32[]{:S(2)}) %collective-permute-start.18) | collective-permute-done | bytes 4194336 | tf_op jit(solution)/shard_map/ppermute | solution.py:183
  826.8 1.8 collective-permute-start.12
  828.6 88.3 %collective-permute-done.17.refs_3_ = bf16[256,8192]{1,0:T(8,128)(2,1)S(1)} collective-permute-done((bf16[256,8192]{1,0:T(8,128)(2,1)}, bf16[256,8192]{1,0:T(8,128)(2,1)S(1)}, u32[]{:S(2)}, u32[]{:S(2)}) %collective-permute-start.17) | collective-permute-done | bytes 4194336 | tf_op jit(solution)/shard_map/ppermute | solution.py:183
  916.9 2.1 collective-permute-start.9
  919.4 18.1 %shard_map.68 = (f32[256,8192]{1,0:T(8,128)}, f32[256,128]{1,0:T(8,128)S(1)}) custom-call(bf16[1024,8192]{1,0:T(8,128)(2,1)} %refs_0_.13, bf16[1024,8192]{1,0:T(8,128)(2,1)} %get-tuple-element.52.refs_5_.refs_1_, bf16[1024,8192]{1,0:T(8,128)(2,1)} %collective-permute-done.refs_2_, bf16[256,1024]{1,0:T(8,128)(2,1)} %collective-permute-done.1.refs_3_, ...), custom_call_target="tpu_custom_call" | custom-call | flops 16777216 | bytes 29360128 | tf_op jit(solution)/shard_map/pallas_call | solution.py:112
  937.5 8.9 shard_map.69
  946.4 1.2 shard_map.70.refs_0_
  947.6 17.6 %shard_map.71 = (f32[256,8192]{1,0:T(8,128)}, f32[256,128]{1,0:T(8,128)S(1)}) custom-call(bf16[1024,8192]{1,0:T(8,128)(2,1)} %refs_0_.13, bf16[1024,8192]{1,0:T(8,128)(2,1)} %get-tuple-element.52.refs_5_.refs_1_, bf16[1024,8192]{1,0:T(8,128)(2,1)} %collective-permute-done.refs_2_, bf16[256,8192]{1,0:T(8,128)(2,1)} %copy-done.4, bf16[256,8192]{1,0:T(8,128)(2,1)} %copy-done.2, ...), custom_call_target="tpu_custom_call" | custom-call | flops 16777216 | bytes 29360128 | tf_op jit(solution)/shard_map/pallas_call | solution.py:112
  965.2 9.0 shard_map.72
  974.2 19.9 %shard_map.73 = (f32[256,8192]{1,0:T(8,128)}, f32[256,128]{1,0:T(8,128)S(1)}) custom-call(bf16[1024,8192]{1,0:T(8,128)(2,1)} %refs_0_.13, bf16[1024,8192]{1,0:T(8,128)(2,1)} %get-tuple-element.52.refs_5_.refs_1_, bf16[1024,8192]{1,0:T(8,128)(2,1)} %collective-permute-done.refs_2_, bf16[256,8192]{1,0:T(8,128)(2,1)} %copy-done.5, bf16[256,8192]{1,0:T(8,128)(2,1)} %copy-done.3, ...), custom_call_target="tpu_custom_call" | custom-call | flops 16777216 | bytes 29360128 | tf_op jit(solution)/shard_map/pallas_call | solution.py:112
  994.0 9.0 shard_map.74
  1003.0 9.2 shard_map.75
  1012.2 4.8 shard_map.76
  1017.0 9.6 shard_map.77
  1026.6 1.7 copy-done
  1028.3 2.6 shard_map.78
  1030.9 5.0 shard_map.79
  1036.0 1.1 shard_map.80
  1037.1 4.7 shard_map.81
  1041.8 0.9 shard_map.82
  (36 shorter events, 0.5 us)
Async XLA Ops:
  254.6 664.5 %collective-permute-start = (bf16[1024,8192]{1,0:T(8,128)(2,1)}, bf16[1024,8192]{1,0:T(8,128)(2,1)}, u32[]{:S(2)}, u32[]{:S(2)}) collective-permute-start(bf16[1024,8192]{1,0:T(8,128)(2,1)} %get-tuple-element.53), channel_id=1, source_target_pairs={{0,1},{1,0},{2,3},{3,2},{4,5},{5,4},{6,7},{7,6}} | collective-permute-start | bytes 50331656 | tf_op jit(solution)/shard_map/ppermute | solution.py:183
  255.4 46.6 %collective-permute-start.5 = (bf16[256,1024]{1,0:T(8,128)(2,1)}, bf16[256,1024]{1,0:T(8,128)(2,1)}, u32[]{:S(2)}, u32[]{:S(2)}) collective-permute-start(bf16[256,1024]{1,0:T(8,128)(2,1)} %shard_map.60.refs_5_), channel_id=1, source_target_pairs={{0,3},{1,2},{2,1},{3,0},{4,7},{5,6},{6,5},{7,4}} | collective-permute-start | bytes 1572872 | tf_op jit(solution)/shard_map/ppermute | solution.py:183
  258.0 44.8 %collective-permute-start.1 = (bf16[256,1024]{1,0:T(8,128)(2,1)}, bf16[256,1024]{1,0:T(8,128)(2,1)}, u32[]{:S(2)}, u32[]{:S(2)}) collective-permute-start(bf16[256,1024]{1,0:T(8,128)(2,1)} %shard_map.59.refs_3_), channel_id=1, source_target_pairs={{0,2},{1,3},{2,0},{3,1},{4,6},{5,7},{6,4},{7,5}} | collective-permute-start | bytes 1572872 | tf_op jit(solution)/shard_map/ppermute | solution.py:183
  258.0 89.8 %collective-permute-start.2 = (bf16[256,1536]{1,0:T(8,128)(2,1)}, bf16[256,1536]{1,0:T(8,128)(2,1)}, u32[]{:S(2)}, u32[]{:S(2)}) collective-permute-start(bf16[256,1536]{1,0:T(8,128)(2,1)} %get-tuple-element.48.refs_5_), channel_id=1, source_target_pairs={{0,2},{1,3},{2,0},{3,1},{4,6},{5,7},{6,4},{7,5}} | collective-permute-start | bytes 2359304 | tf_op jit(solution)/shard_map/ppermute | solution.py:183
  260.0 113.6 %collective-permute-start.3 = (bf16[256,2560]{1,0:T(8,128)(2,1)}, bf16[256,2560]{1,0:T(8,128)(2,1)}, u32[]{:S(2)}, u32[]{:S(2)}) collective-permute-start(bf16[256,2560]{1,0:T(8,128)(2,1)} %get-tuple-element.49.refs_5_), channel_id=1, source_target_pairs={{0,2},{1,3},{2,0},{3,1},{4,6},{5,7},{6,4},{7,5}} | collective-permute-start | bytes 3932168 | tf_op jit(solution)/shard_map/ppermute | solution.py:183
  302.0 43.8 %collective-permute-start.6 = (bf16[256,1536]{1,0:T(8,128)(2,1)}, bf16[256,1536]{1,0:T(8,128)(2,1)}, u32[]{:S(2)}, u32[]{:S(2)}) collective-permute-start(bf16[256,1536]{1,0:T(8,128)(2,1)} %get-tuple-element.54), channel_id=1, source_target_pairs={{0,3},{1,2},{2,1},{3,0},{4,7},{5,6},{6,5},{7,4}} | collective-permute-start | bytes 2359304 | tf_op jit(solution)/shard_map/ppermute | solution.py:183
  302.8 69.0 %collective-permute-start.7 = (bf16[256,2560]{1,0:T(8,128)(2,1)}, bf16[256,2560]{1,0:T(8,128)(2,1)}, u32[]{:S(2)}, u32[]{:S(2)}) collective-permute-start(bf16[256,2560]{1,0:T(8,128)(2,1)} %get-tuple-element.55), channel_id=1, source_target_pairs={{0,3},{1,2},{2,1},{3,0},{4,7},{5,6},{6,5},{7,4}} | collective-permute-start | bytes 3932168 | tf_op jit(solution)/shard_map/ppermute | solution.py:183
  345.8 54.3 %collective-permute-start.13 = (bf16[80,8192]{1,0:T(8,128)(2,1)}, bf16[80,8192]{1,0:T(8,128)(2,1)S(1)}, u32[]{:S(2)}, u32[]{:S(2)}) collective-permute-start(bf16[80,8192]{1,0:T(8,128)(2,1)} %get-tuple-element.66), channel_id=1, source_target_pairs={{0,2},{1,3},{2,0},{3,1},{4,6},{5,7},{6,4},{7,5}} | collective-permute-start | bytes 3932168 | tf_op jit(solution)/shard_map/ppermute | solution.py:183
  347.9 85.7 %collective-permute-start.8 = (bf16[256,3072]{1,0:T(8,128)(2,1)}, bf16[256,3072]{1,0:T(8,128)(2,1)S(1)}, u32[]{:S(2)}, u32[]{:S(2)}) collective-permute-start(bf16[256,3072]{1,0:T(8,128)(2,1)} %get-tuple-element.56), channel_id=1, source_target_pairs={{0,3},{1,2},{2,1},{3,0},{4,7},{5,6},{6,5},{7,4}} | collective-permute-start | bytes 4718600 | tf_op jit(solution)/shard_map/ppermute | solution.py:183
  371.8 187.8 %collective-permute-start.16 = (bf16[128,8192]{1,0:T(8,128)(2,1)}, bf16[128,8192]{1,0:T(8,128)(2,1)S(1)}, u32[]{:S(2)}, u32[]{:S(2)}) collective-permute-start(bf16[128,8192]{1,0:T(8,128)(2,1)} %get-tuple-element.68), channel_id=1, source_target_pairs={{0,3},{1,2},{2,1},{3,0},{4,7},{5,6},{6,5},{7,4}} | collective-permute-start | bytes 6291464 | tf_op jit(solution)/shard_map/ppermute | solution.py:183
  373.7 187.2 %collective-permute-start.15 = (bf16[128,8192]{1,0:T(8,128)(2,1)}, bf16[128,8192]{1,0:T(8,128)(2,1)S(1)}, u32[]{:S(2)}, u32[]{:S(2)}) collective-permute-start(bf16[128,8192]{1,0:T(8,128)(2,1)} %get-tuple-element.58.refs_11_), channel_id=1, source_target_pairs={{0,2},{1,3},{2,0},{3,1},{4,6},{5,7},{6,4},{7,5}} | collective-permute-start | bytes 6291464 | tf_op jit(solution)/shard_map/ppermute | solution.py:183
  400.1 157.3 %collective-permute-start.4 = (bf16[256,3072]{1,0:T(8,128)(2,1)}, bf16[256,3072]{1,0:T(8,128)(2,1)S(1)}, u32[]{:S(2)}, u32[]{:S(2)}) collective-permute-start(bf16[256,3072]{1,0:T(8,128)(2,1)} %get-tuple-element.50.refs_5_), channel_id=1, source_target_pairs={{0,2},{1,3},{2,0},{3,1},{4,6},{5,7},{6,4},{7,5}} | collective-permute-start | bytes 4718600 | tf_op jit(solution)/shard_map/ppermute | solution.py:183
  433.6 485.8 %copy-start.7 = (bf16[256,3072]{1,0:T(8,128)(2,1)}, bf16[256,3072]{1,0:T(8,128)(2,1)S(1)}, u32[]{:S(2)}) copy-start(bf16[256,3072]{1,0:T(8,128)(2,1)S(1)} %collective-permute-done.8.refs_10_) | copy-start | bytes 4718596
  433.6 213.5 %collective-permute-start.20 = (bf16[256,8192]{1,0:T(8,128)(2,1)}, bf16[256,8192]{1,0:T(8,128)(2,1)S(1)}, u32[]{:S(2)}, u32[]{:S(2)}) collective-permute-start(bf16[256,8192]{1,0:T(8,128)(2,1)} %get-tuple-element.70), channel_id=1, source_target_pairs={{0,3},{1,2},{2,1},{3,0},{4,7},{5,6},{6,5},{7,4}} | collective-permute-start | bytes 12582920 | tf_op jit(solution)/shard_map/ppermute | solution.py:183
  557.4 361.7 %copy-start.8 = (bf16[256,3072]{1,0:T(8,128)(2,1)}, bf16[256,3072]{1,0:T(8,128)(2,1)S(1)}, u32[]{:S(2)}) copy-start(bf16[256,3072]{1,0:T(8,128)(2,1)S(1)} %collective-permute-done.4.refs_6_) | copy-start | bytes 4718596
  557.4 179.8 %collective-permute-start.19 = (bf16[256,8192]{1,0:T(8,128)(2,1)}, bf16[256,8192]{1,0:T(8,128)(2,1)S(1)}, u32[]{:S(2)}, u32[]{:S(2)}) collective-permute-start(bf16[256,8192]{1,0:T(8,128)(2,1)} %get-tuple-element.51.refs_5_), channel_id=1, source_target_pairs={{0,2},{1,3},{2,0},{3,1},{4,6},{5,7},{6,4},{7,5}} | collective-permute-start | bytes 12582920 | tf_op jit(solution)/shard_map/ppermute | solution.py:183
  559.5 1.4 copy-start.6
  560.9 265.9 %collective-permute-start.18 = (bf16[256,8192]{1,0:T(8,128)(2,1)}, bf16[256,8192]{1,0:T(8,128)(2,1)S(1)}, u32[]{:S(2)}, u32[]{:S(2)}) collective-permute-start(bf16[256,8192]{1,0:T(8,128)(2,1)} %get-tuple-element.69), channel_id=1, source_target_pairs={{0,3},{1,2},{2,1},{3,0},{4,7},{5,6},{6,5},{7,4}} | collective-permute-start | bytes 12582920 | tf_op jit(solution)/shard_map/ppermute | solution.py:183
  560.9 356.0 %collective-permute-start.17 = (bf16[256,8192]{1,0:T(8,128)(2,1)}, bf16[256,8192]{1,0:T(8,128)(2,1)S(1)}, u32[]{:S(2)}, u32[]{:S(2)}) collective-permute-start(bf16[256,8192]{1,0:T(8,128)(2,1)} %get-tuple-element.57.refs_5_), channel_id=1, source_target_pairs={{0,2},{1,3},{2,0},{3,1},{4,6},{5,7},{6,4},{7,5}} | collective-permute-start | bytes 12582920 | tf_op jit(solution)/shard_map/ppermute | solution.py:183
  647.0 290.4 %copy-start.2 = (bf16[256,8192]{1,0:T(8,128)(2,1)}, bf16[256,8192]{1,0:T(8,128)(2,1)S(1)}, u32[]{:S(2)}) copy-start(bf16[256,8192]{1,0:T(8,128)(2,1)S(1)} %collective-permute-done.20.refs_4_) | copy-start | bytes 12582916
  647.0 369.9 %collective-permute-start.14 = (bf16[80,8192]{1,0:T(8,128)(2,1)}, bf16[80,8192]{1,0:T(8,128)(2,1)S(1)}, u32[]{:S(2)}, u32[]{:S(2)}) collective-permute-start(bf16[80,8192]{1,0:T(8,128)(2,1)} %get-tuple-element.67), channel_id=1, source_target_pairs={{0,3},{1,2},{2,1},{3,0},{4,7},{5,6},{6,5},{7,4}} | collective-permute-start | bytes 3932168 | tf_op jit(solution)/shard_map/ppermute | solution.py:183
  737.2 181.9 %copy-start.4 = (bf16[256,8192]{1,0:T(8,128)(2,1)}, bf16[256,8192]{1,0:T(8,128)(2,1)S(1)}, u32[]{:S(2)}) copy-start(bf16[256,8192]{1,0:T(8,128)(2,1)S(1)} %collective-permute-done.19.refs_3_) | copy-start | bytes 12582916
  737.2 293.8 %collective-permute-start.11 = (bf16[32,8192]{1,0:T(8,128)(2,1)}, bf16[32,8192]{1,0:T(8,128)(2,1)}, u32[]{:S(2)}, u32[]{:S(2)}) collective-permute-start(bf16[32,8192]{1,0:T(8,128)(2,1)} %get-tuple-element.64), channel_id=1, source_target_pairs={{0,2},{1,3},{2,0},{3,1},{4,6},{5,7},{6,4},{7,5}} | collective-permute-start | bytes 1572872 | tf_op jit(solution)/shard_map/ppermute | solution.py:183
  826.8 92.3 %copy-start.3 = (bf16[256,8192]{1,0:T(8,128)(2,1)}, bf16[256,8192]{1,0:T(8,128)(2,1)S(1)}, u32[]{:S(2)}) copy-start(bf16[256,8192]{1,0:T(8,128)(2,1)S(1)} %collective-permute-done.18.refs_4_) | copy-start | bytes 12582916
  826.8 204.1 %collective-permute-start.12 = (bf16[32,8192]{1,0:T(8,128)(2,1)}, bf16[32,8192]{1,0:T(8,128)(2,1)}, u32[]{:S(2)}, u32[]{:S(2)}) collective-permute-start(bf16[32,8192]{1,0:T(8,128)(2,1)} %get-tuple-element.65), channel_id=1, source_target_pairs={{0,3},{1,2},{2,1},{3,0},{4,7},{5,6},{6,5},{7,4}} | collective-permute-start | bytes 1572872 | tf_op jit(solution)/shard_map/ppermute | solution.py:183
  916.9 2.2 copy-start.5
  916.9 120.1 %collective-permute-start.9 = (bf16[16,8192]{1,0:T(8,128)(2,1)}, bf16[16,8192]{1,0:T(8,128)(2,1)}, u32[]{:S(2)}, u32[]{:S(2)}) collective-permute-start(bf16[16,8192]{1,0:T(8,128)(2,1)} %get-tuple-element.62), channel_id=1, source_target_pairs={{0,2},{1,3},{2,0},{3,1},{4,6},{5,7},{6,4},{7,5}} | collective-permute-start | bytes 786440 | tf_op jit(solution)/shard_map/ppermute | solution.py:183
  919.1 18.4 %copy-start.1 = (f32[8192]{0:T(1024)S(1)}, f32[8192]{0:T(1024)}, u32[]{:S(2)}) copy-start(f32[8192]{0:T(1024)} %param.7) | copy-start | bytes 98308
  919.1 118.0 %collective-permute-start.10 = (bf16[16,8192]{1,0:T(8,128)(2,1)}, bf16[16,8192]{1,0:T(8,128)(2,1)}, u32[]{:S(2)}, u32[]{:S(2)}) collective-permute-start(bf16[16,8192]{1,0:T(8,128)(2,1)} %get-tuple-element.63), channel_id=1, source_target_pairs={{0,3},{1,2},{2,1},{3,0},{4,7},{5,6},{6,5},{7,4}} | collective-permute-start | bytes 786440 | tf_op jit(solution)/shard_map/ppermute | solution.py:183
  1026.6 1.7 copy-start

commit v4 on v3

--- a/solution.py
+++ b/solution.py
@@ -14,19 +14,118 @@
 PARAMS = pltpu.CompilerParams(vmem_limit_bytes=VMEM_BYTES)
 SMALL_VMEM = 50 * 2**20
 
+HEAD_ROWS = 256
+HEAD_TILE = 256
+HEAD_LAG = 6
 BOTH = (2, 3)
 PLAN = (
-    ((2,), 0, 256, 0, 1024, 256, (256,)),
-    ((3,), 0, 256, 0, 1024, 256, (256,)),
-    (BOTH, 0, 256, 1024, 1536, 512, (256,)),
-    (BOTH, 0, 256, 2560, 2560, 512, (256,)),
-    (BOTH, 0, 256, 5120, 3072, 512, (256,)),
-    (BOTH, 256, 256, 0, 8192, 512, (256,)),
-    (BOTH, 512, 256, 0, 8192, 512, (256,)),
-    (BOTH, 768, 256, 0, 8192, 512, (128, 80, 32, 16)),
+    ((3,), 0, 256, (256,)),
+    ((3,), 256, 256, (256,)),
+    (BOTH, 512, 256, (256,)),
+    (BOTH, 768, 256, (128, 80, 32, 16)),
 )
-NEAR_AT = 6
+NEAR_AT = 2
 NEAR_ROWS = 256
+
+
+def head(attn, w, tp, rows_total, collective_id):
+    depth, cols = w.shape
+    tiles = cols // HEAD_TILE
+
+    def far():
+        return lax.rem(lax.axis_index("tp") + 2, tp)
+
+    def body(a_ref, w_ref, got_ref, y_ref, held, send_sem, recv_sem):
+        j = pl.program_id(0)
+        peer = {"tp": far()}
+        lag = (1 - lax.rem(lax.axis_index("tp"), 2)) * HEAD_LAG
+
+        def copy(t, row=0, rows=HEAD_ROWS, sem=None):
+            sem = t if sem is None else sem
+            return pltpu.make_async_remote_copy(
+                src_ref=held.at[t, pl.ds(row, rows)],
+                dst_ref=got_ref.at[pl.ds(row, rows), pl.ds(pl.multiple_of(t * HEAD_TILE, HEAD_TILE), HEAD_TILE)],
+                send_sem=send_sem.at[sem],
+                recv_sem=recv_sem.at[sem],
+                device_id=peer,
+                device_id_type=pl.DeviceIdType.MESH,
+            )
+
+        half = HEAD_ROWS // 2
+        upper, lower = copy(0, 0, half, 0), copy(0, half, half, tiles)
+        barrier = pltpu.get_barrier_semaphore()
+
+        @pl.when(j == 0)
+        def _():
+            pl.semaphore_signal(barrier, inc=1, device_id=peer, device_id_type=pl.DeviceIdType.MESH)
+
+        val = jnp.dot(a_ref[:half], w_ref[...], preferred_element_type=F32).astype(BF16)
+
+        @pl.when(j == 0)
+        def _():
+            pl.semaphore_wait(barrier, 1)
+
+        @pl.when(j < tiles)
+        def _():
+            held[j, :half] = val
+
+        @pl.when(j >= tiles)
+        def _():
+            y_ref[:half] = val
+
+        @pl.when((j == 0) & (lag == 0))
+        def _():
+            upper.start()
+
+        val2 = jnp.dot(a_ref[half:], w_ref[...], preferred_element_type=F32).astype(BF16)
+
+        @pl.when(j < tiles)
+        def _():
+            held[j, half:] = val2
+
+            @pl.when((j == 0) & (lag == 0))
+            def _():
+                lower.start()
+
+            @pl.when((j > 0) & (j == lag))
+            def _():
+                upper.start()
+                lower.start()
+                lax.fori_loop(1, lag, lambda t, c: (copy(t).start(), c)[1], 0)
+
+            @pl.when((j > 0) & (j >= lag))
+            def _():
+                copy(j).start()
+
+        @pl.when(j >= tiles)
+        def _():
+            y_ref[half:] = val2
+
+        @pl.when(j == 2 * tiles - 1)
+        def _():
+            upper.wait()
+            lower.wait()
+            lax.fori_loop(1, tiles, lambda t, c: (copy(t).wait(), c)[1], 0)
+
+    per = rows_total // HEAD_ROWS
+    return pl.pallas_call(
+        body,
+        grid=(2 * tiles,),
+        in_specs=[
+            pl.BlockSpec((HEAD_ROWS, depth), lambda j: (far() * per + j // tiles, 0)),
+            pl.BlockSpec((depth, HEAD_TILE), lambda j: (0, lax.rem(j, tiles))),
+        ],
+        out_specs=[ANY, pl.BlockSpec((HEAD_ROWS, HEAD_TILE), lambda j: (0, jnp.maximum(j - tiles, 0)))],
+        out_shape=[jax.ShapeDtypeStruct((HEAD_ROWS, cols), BF16)] * 2,
+        scratch_shapes=[
+            pltpu.VMEM((tiles, HEAD_ROWS, HEAD_TILE), BF16),
+            pltpu.SemaphoreType.DMA((tiles + 1,)),
+            pltpu.SemaphoreType.DMA((tiles + 1,)),
+        ],
+        compiler_params=pltpu.CompilerParams(vmem_limit_bytes=VMEM_BYTES, collective_id=collective_id, has_side_effects=True),
+        cost_estimate=pl.CostEstimate(flops=4 * HEAD_ROWS * depth * cols, bytes_accessed=4 * depth * cols, transcendentals=0),
+        name="head",
+    )(attn, w)
 
 
 def products(attn, w, blocks, reps, tm, col0, ncols, tn, splits, deps):
@@ -186,22 +285,25 @@
         me = lax.axis_index("tp")
         rows_total, cols = res.shape
         pieces = {}
-        dep = []
         near = None
 
-        for t, (flips, row, tm, col0, ncols, tn, splits) in enumerate(PLAN):
+        got, y = head(attn, w, tp, rows_total, 7)
+        pieces[0, HEAD_ROWS] = ([got], [])
+        pieces[HEAD_ROWS, HEAD_ROWS] = ([send(y, 2)], [])
+        dep = [y]
+        for t, (flips, row, tm, splits) in enumerate(PLAN):
             if t == NEAR_AT:
                 reps = rows_total // NEAR_ROWS
                 other, own = products(attn, w, [(me ^ 1) * reps, me * reps], reps, NEAR_ROWS, 0, cols, 1024, (NEAR_ROWS,), dep)
                 dep = [own]
                 near = [own, send(other, 1)]
             per = rows_total // tm
-            outs = products(attn, w, [(me ^ flip) * per + row // tm for flip in flips], 1, tm, col0, ncols, tn, splits, dep)
+            outs = products(attn, w, [(me ^ flip) * per + row // tm for flip in flips], 1, tm, 0, cols, 512, splits, dep)
             dep = [outs[0]]
             for s, size in enumerate(splits):
-                got = pieces.setdefault((row, size), ([], []))
+                into = pieces.setdefault((row, size), ([], []))
                 for b, flip in enumerate(flips):
-                    got[BOTH.index(flip)].append(send(outs[b * len(splits) + s], flip))
+                    into[BOTH.index(flip)].append(send(outs[b * len(splits) + s], flip))
                 row += size
 
         gain2 = gain.reshape(1, cols)

time: 1050 us -> 1020 us (0.971)
  waiting for transfers between devices: 554 us -> 478 us
  Pallas kernels: 459 us -> 527 us
  starting transfers between devices: 25.8 us -> 9.68 us
    pallas_call x0 -> x1, Pallas kernels: none -> 105 us  [head(): pl.pallas_call(body, grid=(2 * tiles,), in_specs=[pl.BlockSpec((HEAD_ROWS...]
    ppermute x21 -> x14, waiting for transfers between devices: 554 us -> 478 us  [send(): return lax.ppermute(x, 'tp', [(i, i ^ flip) for i in range(tp)])]
    pallas_call x9 -> x5, Pallas kernels: 338 us -> 301 us  [products(): pl.pallas_call(body, grid_spec=pltpu.PrefetchScalarGridSpec(num_scalar_pr...]
    ppermute x21 -> x14, starting transfers between devices: 25.8 us -> 9.68 us  [send(): return lax.ppermute(x, 'tp', [(i, i ^ flip) for i in range(tp)])]
  transfers between devices with their start and end apart: 21 -> 14, of which waited for: 8 -> 7; matrix products, arithmetic and copies ran while one was open for 0% -> 0% of each run, Pallas kernels for 19% -> 19%
where the time goes in v4:
time: 1020 us
  Pallas kernels  527 us (52%)
  waiting for transfers between devices  478 us (47%)
    ppermute x14, waiting for transfers between devices, send(): return lax.ppermute(x, 'tp', [(i, i ^ flip) for i in range(tp)])  478 us
    pallas_call x5, Pallas kernels, products(): pl.pallas_call(body, grid_spec=pltpu.PrefetchScalarGridSpec(num_scalar_pr...  301 us
    pallas_call x1, Pallas kernels, head(): pl.pallas_call(body, grid=(2 * tiles,), in_specs=[pl.BlockSpec((HEAD_ROWS...  105 us
    pallas_call x7, Pallas kernels, add_rows(): pl.pallas_call(body, grid=(steps,), in_specs=in_specs, out_specs=[pl.Bloc...  82.9 us
    pallas_call x7, Pallas kernels, norm_rows(): pl.pallas_call(body, grid=(rows // tr,), in_specs=in_specs, out_specs=[pl...  36.3 us
  transfers between devices with their start and end apart: 14, of which 7 were waited for; matrix products, arithmetic and copies ran while one was open for 0% of the time, Pallas kernels for 19%

profile of v4, /device:TPU:0, one launch (start us, length us, event | category | flops | bytes accessed | tf_op | source)
XLA Modules:
  0.0 1020.1 jit_solution(12257657016853088460)
XLA Ops:
  0.6 105.4 %head.1 = (bf16[256,8192]{1,0:T(8,128)(2,1)}, bf16[256,8192]{1,0:T(8,128)(2,1)}) custom-call(bf16[4096,4096]{1,0:T(8,128)(2,1)} %refs_3_.5, bf16[4096,8192]{1,0:T(8,128)(2,1)} %refs_4_.5), custom_call_target="tpu_custom_call" | custom-call | flops 34359738368 | bytes 134217728 | tf_op jit(solution)/shard_map/head/pallas_call | solution.py:111
  106.0 32.3 %shard_map.59.refs_3_ = bf16[256,8192]{1,0:T(8,128)(2,1)} custom-call(s32[1]{0:T(128)} %bitcast.3.refs_0_, bf16[4096,4096]{1,0:T(8,128)(2,1)} %refs_3_.5, bf16[4096,8192]{1,0:T(8,128)(2,1)} %refs_4_.5, bf16[256,8192]{1,0:T(8,128)(2,1)} %get-tuple-element.42.refs_3_), custom_call_target="tpu_custom_call" | custom-call | flops 17179869184 | bytes 73400320 | tf_op jit(solution)/shard_map/pallas_call | solution.py:149
  138.3 32.3 %shard_map.60.refs_5_ = bf16[256,8192]{1,0:T(8,128)(2,1)} custom-call(s32[1]{0:T(128)} %bitcast.2.refs_0_, bf16[4096,4096]{1,0:T(8,128)(2,1)} %refs_3_.5, bf16[4096,8192]{1,0:T(8,128)(2,1)} %refs_4_.5, bf16[256,8192]{1,0:T(8,128)(2,1)} %shard_map.59.refs_3_), custom_call_target="tpu_custom_call" | custom-call | flops 17179869184 | bytes 73400320 | tf_op jit(solution)/shard_map/pallas_call | solution.py:149
  170.5 152.4 %shard_map.61 = (bf16[1024,8192]{1,0:T(8,128)(2,1)}, bf16[1024,8192]{1,0:T(8,128)(2,1)}) custom-call(s32[1]{0:T(128)} %bitcast.refs_0_, s32[1]{0:T(128)} %bitcast.1.refs_1_, bf16[4096,4096]{1,0:T(8,128)(2,1)} %refs_3_.5, bf16[4096,4096]{1,0:T(8,128)(2,1)} %refs_3_.5, bf16[4096,8192]{1,0:T(8,128)(2,1)} %refs_4_.5, bf16[256,8192]{1,0:T(8,128)(2,1)} %shard_map.60.refs_5_), custom_call_target="tpu_custom_call" | custom-call | flops 137438953472 | bytes 117440512 | tf_op jit(solution)/shard_map/pallas_call | solution.py:149
  323.0 0.0 collective-permute-start
  323.0 0.8 collective-permute-start.13
  323.8 41.9 %shard_map.62 = (bf16[256,8192]{1,0:T(8,128)(2,1)}, bf16[256,8192]{1,0:T(8,128)(2,1)}) custom-call(s32[1]{0:T(128)} %bitcast.6.refs_0_, s32[1]{0:T(128)} %bitcast.7.refs_1_, bf16[4096,4096]{1,0:T(8,128)(2,1)} %refs_3_.5, bf16[4096,4096]{1,0:T(8,128)(2,1)} %refs_3_.5, bf16[4096,8192]{1,0:T(8,128)(2,1)} %refs_4_.5, ...), custom_call_target="tpu_custom_call" | custom-call | flops 34359738368 | bytes 79691776 | tf_op jit(solution)/shard_map/pallas_call | solution.py:149
  365.7 42.0 %shard_map.63 = (bf16[128,8192]{1,0:T(8,128)(2,1)}, bf16[80,8192]{1,0:T(8,128)(2,1)}, bf16[32,8192]{1,0:T(8,128)(2,1)}, bf16[16,8192]{1,0:T(8,128)(2,1)}, bf16[1...) custom-call(s32[1]{0:T(128)} %bitcast.4.refs_0_, ...), custom_call_target="tpu_custom_call" | custom-call | flops 34359738368 | bytes 79691776 | tf_op jit(solution)/shard_map/pallas_call | solution.py:149
  407.7 1.3 collective-permute-start.6
  409.1 0.0 collective-permute-start.9
  409.1 1.3 collective-permute-start.8
  410.4 34.4 %collective-permute-done.6.refs_3_ = bf16[80,8192]{1,0:T(8,128)(2,1)S(1)} collective-permute-done((bf16[80,8192]{1,0:T(8,128)(2,1)}, bf16[80,8192]{1,0:T(8,128)(2,1)S(1)}, u32[]{:S(2)}, u32[]{:S(2)}) %collective-permute-start.6) | collective-permute-done | bytes 1310752 | tf_op jit(solution)/shard_map/ppermute | solution.py:282
  444.8 0.0 collective-permute-start.1
  444.8 43.6 %collective-permute-done.9.refs_4_ = bf16[128,8192]{1,0:T(8,128)(2,1)S(1)} collective-permute-done((bf16[128,8192]{1,0:T(8,128)(2,1)}, bf16[128,8192]{1,0:T(8,128)(2,1)S(1)}, u32[]{:S(2)}, u32[]{:S(2)}) %collective-permute-start.9) | collective-permute-done | bytes 2097184 | tf_op jit(solution)/shard_map/ppermute | solution.py:282
  488.4 1.0 collective-permute-start.12
  489.4 45.3 %collective-permute-done.8.refs_3_ = bf16[128,8192]{1,0:T(8,128)(2,1)S(1)} collective-permute-done((bf16[128,8192]{1,0:T(8,128)(2,1)}, bf16[128,8192]{1,0:T(8,128)(2,1)S(1)}, u32[]{:S(2)}, u32[]{:S(2)}) %collective-permute-start.8) | collective-permute-done | bytes 2097184 | tf_op jit(solution)/shard_map/ppermute | solution.py:282
  534.7 0.0 collective-permute-start.11
  534.7 0.0 collective-permute-done.13.refs_4_
  534.7 0.7 collective-permute-start.10
  535.4 87.8 %collective-permute-done.1.refs_4_ = bf16[256,8192]{1,0:T(8,128)(2,1)S(1)} collective-permute-done((bf16[256,8192]{1,0:T(8,128)(2,1)}, bf16[256,8192]{1,0:T(8,128)(2,1)S(1)}, u32[]{:S(2)}, u32[]{:S(2)}) %collective-permute-start.1) | collective-permute-done | bytes 4194336 | tf_op jit(solution)/shard_map/ppermute | solution.py:282
  623.2 1.5 collective-permute-start.7
  624.7 89.7 %collective-permute-done.12.refs_3_ = bf16[256,8192]{1,0:T(8,128)(2,1)S(1)} collective-permute-done((bf16[256,8192]{1,0:T(8,128)(2,1)}, bf16[256,8192]{1,0:T(8,128)(2,1)S(1)}, u32[]{:S(2)}, u32[]{:S(2)}) %collective-permute-start.12) | collective-permute-done | bytes 4194336 | tf_op jit(solution)/shard_map/ppermute | solution.py:282
  714.5 0.7 collective-permute-start.4
  715.2 87.8 %collective-permute-done.11.refs_4_ = bf16[256,8192]{1,0:T(8,128)(2,1)S(1)} collective-permute-done((bf16[256,8192]{1,0:T(8,128)(2,1)}, bf16[256,8192]{1,0:T(8,128)(2,1)S(1)}, u32[]{:S(2)}, u32[]{:S(2)}) %collective-permute-start.11) | collective-permute-done | bytes 4194336 | tf_op jit(solution)/shard_map/ppermute | solution.py:282
  803.0 1.5 collective-permute-start.5
  804.5 89.7 %collective-permute-done.10.refs_3_ = bf16[256,8192]{1,0:T(8,128)(2,1)S(1)} collective-permute-done((bf16[256,8192]{1,0:T(8,128)(2,1)}, bf16[256,8192]{1,0:T(8,128)(2,1)S(1)}, u32[]{:S(2)}, u32[]{:S(2)}) %collective-permute-start.10) | collective-permute-done | bytes 4194336 | tf_op jit(solution)/shard_map/ppermute | solution.py:282
  894.3 0.7 collective-permute-start.2
  895.0 0.0 collective-permute-done.refs_2_
  895.0 1.3 copy-done.5
  896.3 1.6 copy-done.1
  897.9 18.9 %shard_map.64 = (f32[256,8192]{1,0:T(8,128)}, f32[256,128]{1,0:T(8,128)S(1)}) custom-call(bf16[1024,8192]{1,0:T(8,128)(2,1)} %refs_0_.13, bf16[1024,8192]{1,0:T(8,128)(2,1)} %get-tuple-element.43.refs_5_.refs_1_, bf16[1024,8192]{1,0:T(8,128)(2,1)} %collective-permute-done.refs_2_, bf16[256,8192]{1,0:T(8,128)(2,1)} %get-tuple-element.45.refs_3_, ...), custom_call_target="tpu_custom_call" | custom-call | flops 16777216 | bytes 29360128 | tf_op jit(solution)/shard_map/pallas_call | solution.py:211
  916.8 8.9 shard_map.65
  925.8 1.2 shard_map.66.refs_0_
  927.0 17.3 %shard_map.67 = (f32[256,8192]{1,0:T(8,128)}, f32[256,128]{1,0:T(8,128)S(1)}) custom-call(bf16[1024,8192]{1,0:T(8,128)(2,1)} %refs_0_.13, bf16[1024,8192]{1,0:T(8,128)(2,1)} %get-tuple-element.43.refs_5_.refs_1_, bf16[1024,8192]{1,0:T(8,128)(2,1)} %collective-permute-done.refs_2_, bf16[256,8192]{1,0:T(8,128)(2,1)} %copy-done.4, ...), custom_call_target="tpu_custom_call" | custom-call | flops 16777216 | bytes 29360128 | tf_op jit(solution)/shard_map/pallas_call | solution.py:211
  944.3 9.0 shard_map.68
  953.2 18.1 %shard_map.69 = (f32[256,8192]{1,0:T(8,128)}, f32[256,128]{1,0:T(8,128)S(1)}) custom-call(bf16[1024,8192]{1,0:T(8,128)(2,1)} %refs_0_.13, bf16[1024,8192]{1,0:T(8,128)(2,1)} %get-tuple-element.43.refs_5_.refs_1_, bf16[1024,8192]{1,0:T(8,128)(2,1)} %collective-permute-done.refs_2_, bf16[256,8192]{1,0:T(8,128)(2,1)} %copy-done.5, bf16[256,8192]{1,0:T(8,128)(2,1)} %copy-done.3, ...), custom_call_target="tpu_custom_call" | custom-call | flops 16777216 | bytes 29360128 | tf_op jit(solution)/shard_map/pallas_call | solution.py:211
  971.3 9.1 shard_map.70
  980.4 9.6 shard_map.71
  990.0 4.8 shard_map.72
  994.8 9.3 shard_map.73
  1004.1 1.7 copy-done
  1005.8 2.6 shard_map.74
  1008.4 0.0 collective-permute-done.4.refs_3_
  1008.4 0.0 collective-permute-done.5.refs_4_
  1008.4 5.0 shard_map.75
  1013.5 1.1 shard_map.76
  1014.6 4.7 shard_map.77
  1019.3 0.9 shard_map.78
  (17 shorter events, 0.0 us)
Async XLA Ops:
  323.0 572.0 %collective-permute-start = (bf16[1024,8192]{1,0:T(8,128)(2,1)}, bf16[1024,8192]{1,0:T(8,128)(2,1)}, u32[]{:S(2)}, u32[]{:S(2)}) collective-permute-start(bf16[1024,8192]{1,0:T(8,128)(2,1)} %get-tuple-element.44), channel_id=1, source_target_pairs={{0,1},{1,0},{2,3},{3,2},{4,5},{5,4},{6,7},{7,6}} | collective-permute-start | bytes 50331656 | tf_op jit(solution)/shard_map/ppermute | solution.py:282
  323.0 211.7 %collective-permute-start.13 = (bf16[256,8192]{1,0:T(8,128)(2,1)}, bf16[256,8192]{1,0:T(8,128)(2,1)}, u32[]{:S(2)}, u32[]{:S(2)}) collective-permute-start(bf16[256,8192]{1,0:T(8,128)(2,1)} %shard_map.60.refs_5_), channel_id=1, source_target_pairs={{0,3},{1,2},{2,1},{3,0},{4,7},{5,6},{6,5},{7,4}} | collective-permute-start | bytes 12582920 | tf_op jit(solution)/shard_map/ppermute | solution.py:282
  407.7 37.1 %collective-permute-start.6 = (bf16[80,8192]{1,0:T(8,128)(2,1)}, bf16[80,8192]{1,0:T(8,128)(2,1)S(1)}, u32[]{:S(2)}, u32[]{:S(2)}) collective-permute-start(bf16[80,8192]{1,0:T(8,128)(2,1)} %get-tuple-element.55), channel_id=1, source_target_pairs={{0,2},{1,3},{2,0},{3,1},{4,6},{5,7},{6,4},{7,5}} | collective-permute-start | bytes 3932168 | tf_op jit(solution)/shard_map/ppermute | solution.py:282
  409.1 79.3 %collective-permute-start.9 = (bf16[128,8192]{1,0:T(8,128)(2,1)}, bf16[128,8192]{1,0:T(8,128)(2,1)S(1)}, u32[]{:S(2)}, u32[]{:S(2)}) collective-permute-start(bf16[128,8192]{1,0:T(8,128)(2,1)} %get-tuple-element.57), channel_id=1, source_target_pairs={{0,3},{1,2},{2,1},{3,0},{4,7},{5,6},{6,5},{7,4}} | collective-permute-start | bytes 6291464 | tf_op jit(solution)/shard_map/ppermute | solution.py:282
  409.1 125.6 %collective-permute-start.8 = (bf16[128,8192]{1,0:T(8,128)(2,1)}, bf16[128,8192]{1,0:T(8,128)(2,1)S(1)}, u32[]{:S(2)}, u32[]{:S(2)}) collective-permute-start(bf16[128,8192]{1,0:T(8,128)(2,1)} %get-tuple-element.47.refs_5_), channel_id=1, source_target_pairs={{0,2},{1,3},{2,0},{3,1},{4,6},{5,7},{6,4},{7,5}} | collective-permute-start | bytes 6291464 | tf_op jit(solution)/shard_map/ppermute | solution.py:282
  444.8 178.4 %collective-permute-start.1 = (bf16[256,8192]{1,0:T(8,128)(2,1)}, bf16[256,8192]{1,0:T(8,128)(2,1)S(1)}, u32[]{:S(2)}, u32[]{:S(2)}) collective-permute-start(bf16[256,8192]{1,0:T(8,128)(2,1)} %shard_map.59.refs_3_), channel_id=1, source_target_pairs={{0,3},{1,2},{2,1},{3,0},{4,7},{5,6},{6,5},{7,4}} | collective-permute-start | bytes 12582920 | tf_op jit(solution)/shard_map/ppermute | solution.py:282
  488.4 428.4 %copy-start.7 = (bf16[128,8192]{1,0:T(8,128)(2,1)}, bf16[128,8192]{1,0:T(8,128)(2,1)S(1)}, u32[]{:S(2)}) copy-start(bf16[128,8192]{1,0:T(8,128)(2,1)S(1)} %collective-permute-done.9.refs_4_) | copy-start | bytes 6291460
  488.4 226.1 %collective-permute-start.12 = (bf16[256,8192]{1,0:T(8,128)(2,1)}, bf16[256,8192]{1,0:T(8,128)(2,1)S(1)}, u32[]{:S(2)}, u32[]{:S(2)}) collective-permute-start(bf16[256,8192]{1,0:T(8,128)(2,1)} %get-tuple-element.42.refs_3_), channel_id=1, source_target_pairs={{0,2},{1,3},{2,0},{3,1},{4,6},{5,7},{6,4},{7,5}} | collective-permute-start | bytes 12582920 | tf_op jit(solution)/shard_map/ppermute | solution.py:282
  534.7 268.3 %collective-permute-start.11 = (bf16[256,8192]{1,0:T(8,128)(2,1)}, bf16[256,8192]{1,0:T(8,128)(2,1)S(1)}, u32[]{:S(2)}, u32[]{:S(2)}) collective-permute-start(bf16[256,8192]{1,0:T(8,128)(2,1)} %get-tuple-element.58), channel_id=1, source_target_pairs={{0,3},{1,2},{2,1},{3,0},{4,7},{5,6},{6,5},{7,4}} | collective-permute-start | bytes 12582920 | tf_op jit(solution)/shard_map/ppermute | solution.py:282
  534.7 359.5 %collective-permute-start.10 = (bf16[256,8192]{1,0:T(8,128)(2,1)}, bf16[256,8192]{1,0:T(8,128)(2,1)S(1)}, u32[]{:S(2)}, u32[]{:S(2)}) collective-permute-start(bf16[256,8192]{1,0:T(8,128)(2,1)} %get-tuple-element.46.refs_5_), channel_id=1, source_target_pairs={{0,2},{1,3},{2,0},{3,1},{4,6},{5,7},{6,4},{7,5}} | collective-permute-start | bytes 12582920 | tf_op jit(solution)/shard_map/ppermute | solution.py:282
  623.2 271.7 %copy-start.6 = (bf16[256,8192]{1,0:T(8,128)(2,1)}, bf16[256,8192]{1,0:T(8,128)(2,1)S(1)}, u32[]{:S(2)}) copy-start(bf16[256,8192]{1,0:T(8,128)(2,1)S(1)} %collective-permute-done.1.refs_4_) | copy-start | bytes 12582916
  623.2 371.6 %collective-permute-start.7 = (bf16[80,8192]{1,0:T(8,128)(2,1)}, bf16[80,8192]{1,0:T(8,128)(2,1)S(1)}, u32[]{:S(2)}, u32[]{:S(2)}) collective-permute-start(bf16[80,8192]{1,0:T(8,128)(2,1)} %get-tuple-element.56), channel_id=1, source_target_pairs={{0,3},{1,2},{2,1},{3,0},{4,7},{5,6},{6,5},{7,4}} | collective-permute-start | bytes 3932168 | tf_op jit(solution)/shard_map/ppermute | solution.py:282
  714.5 180.5 %copy-start.4 = (bf16[256,8192]{1,0:T(8,128)(2,1)}, bf16[256,8192]{1,0:T(8,128)(2,1)S(1)}, u32[]{:S(2)}) copy-start(bf16[256,8192]{1,0:T(8,128)(2,1)S(1)} %collective-permute-done.12.refs_3_) | copy-start | bytes 12582916
  714.5 293.9 %collective-permute-start.4 = (bf16[32,8192]{1,0:T(8,128)(2,1)}, bf16[32,8192]{1,0:T(8,128)(2,1)}, u32[]{:S(2)}, u32[]{:S(2)}) collective-permute-start(bf16[32,8192]{1,0:T(8,128)(2,1)} %get-tuple-element.53), channel_id=1, source_target_pairs={{0,2},{1,3},{2,0},{3,1},{4,6},{5,7},{6,4},{7,5}} | collective-permute-start | bytes 1572872 | tf_op jit(solution)/shard_map/ppermute | solution.py:282
  803.0 113.8 %copy-start.3 = (bf16[256,8192]{1,0:T(8,128)(2,1)}, bf16[256,8192]{1,0:T(8,128)(2,1)S(1)}, u32[]{:S(2)}) copy-start(bf16[256,8192]{1,0:T(8,128)(2,1)S(1)} %collective-permute-done.11.refs_4_) | copy-start | bytes 12582916
  803.0 205.4 %collective-permute-start.5 = (bf16[32,8192]{1,0:T(8,128)(2,1)}, bf16[32,8192]{1,0:T(8,128)(2,1)}, u32[]{:S(2)}, u32[]{:S(2)}) collective-permute-start(bf16[32,8192]{1,0:T(8,128)(2,1)} %get-tuple-element.54), channel_id=1, source_target_pairs={{0,3},{1,2},{2,1},{3,0},{4,7},{5,6},{6,5},{7,4}} | collective-permute-start | bytes 1572872 | tf_op jit(solution)/shard_map/ppermute | solution.py:282
  894.3 2.0 copy-start.5
  894.3 120.3 %collective-permute-start.2 = (bf16[16,8192]{1,0:T(8,128)(2,1)}, bf16[16,8192]{1,0:T(8,128)(2,1)}, u32[]{:S(2)}, u32[]{:S(2)}) collective-permute-start(bf16[16,8192]{1,0:T(8,128)(2,1)} %get-tuple-element.51), channel_id=1, source_target_pairs={{0,2},{1,3},{2,0},{3,1},{4,6},{5,7},{6,4},{7,5}} | collective-permute-start | bytes 786440 | tf_op jit(solution)/shard_map/ppermute | solution.py:282
  895.0 119.6 %collective-permute-start.3 = (bf16[16,8192]{1,0:T(8,128)(2,1)}, bf16[16,8192]{1,0:T(8,128)(2,1)}, u32[]{:S(2)}, u32[]{:S(2)}) collective-permute-start(bf16[16,8192]{1,0:T(8,128)(2,1)} %get-tuple-element.52), channel_id=1, source_target_pairs={{0,3},{1,2},{2,1},{3,0},{4,7},{5,6},{6,5},{7,4}} | collective-permute-start | bytes 786440 | tf_op jit(solution)/shard_map/ppermute | solution.py:282
  896.3 1.6 copy-start.1
  897.9 18.9 %copy-start.2 = (f32[8192]{0:T(1024)S(1)}, f32[8192]{0:T(1024)}, u32[]{:S(2)}) copy-start(f32[8192]{0:T(1024)} %param.7) | copy-start | bytes 98308
  1004.1 1.7 copy-start

commit v5 on v4

--- a/solution.py
+++ b/solution.py
@@ -24,7 +24,7 @@
     (BOTH, 512, 256, (256,)),
     (BOTH, 768, 256, (128, 80, 32, 16)),
 )
-NEAR_AT = 2
+NEAR_AT = 3
 NEAR_ROWS = 256
 
 
@@ -40,26 +40,23 @@
         peer = {"tp": far()}
         lag = (1 - lax.rem(lax.axis_index("tp"), 2)) * HEAD_LAG
 
-        def copy(t, row=0, rows=HEAD_ROWS, sem=None):
-            sem = t if sem is None else sem
+        def copy(t):
             return pltpu.make_async_remote_copy(
-                src_ref=held.at[t, pl.ds(row, rows)],
-                dst_ref=got_ref.at[pl.ds(row, rows), pl.ds(pl.multiple_of(t * HEAD_TILE, HEAD_TILE), HEAD_TILE)],
-                send_sem=send_sem.at[sem],
-                recv_sem=recv_sem.at[sem],
+                src_ref=held.at[t],
+                dst_ref=got_ref.at[:, pl.ds(pl.multiple_of(t * HEAD_TILE, HEAD_TILE), HEAD_TILE)],
+                send_sem=send_sem.at[t],
+                recv_sem=recv_sem.at[t],
                 device_id=peer,
                 device_id_type=pl.DeviceIdType.MESH,
             )
 
-        half = HEAD_ROWS // 2
-        upper, lower = copy(0, 0, half, 0), copy(0, half, half, tiles)
         barrier = pltpu.get_barrier_semaphore()
 
         @pl.when(j == 0)
         def _():
             pl.semaphore_signal(barrier, inc=1, device_id=peer, device_id_type=pl.DeviceIdType.MESH)
 
-        val = jnp.dot(a_ref[:half], w_ref[...], preferred_element_type=F32).astype(BF16)
+        val = jnp.dot(a_ref[...], w_ref[...], preferred_element_type=F32).astype(BF16)
 
         @pl.when(j == 0)
         def _():
@@ -67,45 +64,23 @@
 
         @pl.when(j < tiles)
         def _():
-            held[j, :half] = val
-
-        @pl.when(j >= tiles)
-        def _():
-            y_ref[:half] = val
-
-        @pl.when((j == 0) & (lag == 0))
-        def _():
-            upper.start()
-
-        val2 = jnp.dot(a_ref[half:], w_ref[...], preferred_element_type=F32).astype(BF16)
-
-        @pl.when(j < tiles)
-        def _():
-            held[j, half:] = val2
-
-            @pl.when((j == 0) & (lag == 0))
+            held[j] = val
+
+            @pl.when(j == lag)
             def _():
-                lower.start()
-
-            @pl.when((j > 0) & (j == lag))
-            def _():
-                upper.start()
-                lower.start()
-                lax.fori_loop(1, lag, lambda t, c: (copy(t).start(), c)[1], 0)
-
-            @pl.when((j > 0) & (j >= lag))
+                lax.fori_loop(0, lag, lambda t, c: (copy(t).start(), c)[1], 0)
+
+            @pl.when(j >= lag)
             def _():
                 copy(j).start()
 
         @pl.when(j >= tiles)
         def _():
-            y_ref[half:] = val2
+            y_ref[...] = val
 
         @pl.when(j == 2 * tiles - 1)
         def _():
-            upper.wait()
-            lower.wait()
-            lax.fori_loop(1, tiles, lambda t, c: (copy(t).wait(), c)[1], 0)
+            lax.fori_loop(0, tiles, lambda t, c: (copy(t).wait(), c)[1], 0)
 
     per = rows_total // HEAD_ROWS
     return pl.pallas_call(
@@ -119,8 +94,8 @@
         out_shape=[jax.ShapeDtypeStruct((HEAD_ROWS, cols), BF16)] * 2,
         scratch_shapes=[
             pltpu.VMEM((tiles, HEAD_ROWS, HEAD_TILE), BF16),
-            pltpu.SemaphoreType.DMA((tiles + 1,)),
-            pltpu.SemaphoreType.DMA((tiles + 1,)),
+            pltpu.SemaphoreType.DMA((tiles,)),
+            pltpu.SemaphoreType.DMA((tiles,)),
         ],
         compiler_params=pltpu.CompilerParams(vmem_limit_bytes=VMEM_BYTES, collective_id=collective_id, has_side_effects=True),
         cost_estimate=pl.CostEstimate(flops=4 * HEAD_ROWS * depth * cols, bytes_accessed=4 * depth * cols, transcendentals=0),

time: 1020 us -> 1060 us (1.039)
  waiting for transfers between devices: 478 us -> 519 us
    ppermute x14, waiting for transfers between devices: 478 us -> 519 us  [send(): return lax.ppermute(x, 'tp', [(i, i ^ flip) for i in range(tp)])]
  transfers between devices with their start and end apart: 14 -> 14, of which waited for: 7 -> 7; matrix products, arithmetic and copies ran while one was open for 0% -> 0% of each run, Pallas kernels for 19% -> 15%
where the time goes in v5:
time: 1060 us; the launch traced here: 1050 us
  Pallas kernels  520 us (49%)
  waiting for transfers between devices  519 us (49%)
  starting transfers between devices  11.2 us (1%)
    ppermute x14, waiting for transfers between devices, send(): return lax.ppermute(x, 'tp', [(i, i ^ flip) for i in range(tp)])  519 us
    pallas_call x5, Pallas kernels, products(): pl.pallas_call(body, grid_spec=pltpu.PrefetchScalarGridSpec(num_scalar_pr...  301 us
    pallas_call x1, Pallas kernels, head(): pl.pallas_call(body, grid=(2 * tiles,), in_specs=[pl.BlockSpec((HEAD_ROWS...  98.2 us
    pallas_call x7, Pallas kernels, add_rows(): pl.pallas_call(body, grid=(steps,), in_specs=in_specs, out_specs=[pl.Bloc...  83.1 us
    pallas_call x7, Pallas kernels, norm_rows(): pl.pallas_call(body, grid=(rows // tr,), in_specs=in_specs, out_specs=[pl...  36.2 us
  transfers between devices with their start and end apart: 14, of which 7 were waited for; matrix products, arithmetic and copies ran while one was open for 0% of the time, Pallas kernels for 15%

profile of v5, /device:TPU:0, one launch (start us, length us, event | category | flops | bytes accessed | tf_op | source)
XLA Modules:
  0.0 1054.9 jit_solution(13245831428797804267)
XLA Ops:
  0.6 98.2 %head.1 = (bf16[256,8192]{1,0:T(8,128)(2,1)}, bf16[256,8192]{1,0:T(8,128)(2,1)}) custom-call(bf16[4096,4096]{1,0:T(8,128)(2,1)} %refs_3_.5, bf16[4096,8192]{1,0:T(8,128)(2,1)} %refs_4_.5), custom_call_target="tpu_custom_call" | custom-call | flops 34359738368 | bytes 134217728 | tf_op jit(solution)/shard_map/head/pallas_call | solution.py:86
  98.9 32.3 %shard_map.59.refs_3_ = bf16[256,8192]{1,0:T(8,128)(2,1)} custom-call(s32[1]{0:T(128)} %bitcast.5.refs_0_, bf16[4096,4096]{1,0:T(8,128)(2,1)} %refs_3_.5, bf16[4096,8192]{1,0:T(8,128)(2,1)} %refs_4_.5, bf16[256,8192]{1,0:T(8,128)(2,1)} %get-tuple-element.42.refs_3_), custom_call_target="tpu_custom_call" | custom-call | flops 17179869184 | bytes 73400320 | tf_op jit(solution)/shard_map/pallas_call | solution.py:124
  131.1 32.3 %shard_map.60.refs_5_ = bf16[256,8192]{1,0:T(8,128)(2,1)} custom-call(s32[1]{0:T(128)} %bitcast.4.refs_0_, bf16[4096,4096]{1,0:T(8,128)(2,1)} %refs_3_.5, bf16[4096,8192]{1,0:T(8,128)(2,1)} %refs_4_.5, bf16[256,8192]{1,0:T(8,128)(2,1)} %shard_map.59.refs_3_), custom_call_target="tpu_custom_call" | custom-call | flops 17179869184 | bytes 73400320 | tf_op jit(solution)/shard_map/pallas_call | solution.py:124
  163.4 41.9 %shard_map.61 = (bf16[256,8192]{1,0:T(8,128)(2,1)}, bf16[256,8192]{1,0:T(8,128)(2,1)}) custom-call(s32[1]{0:T(128)} %bitcast.2.refs_0_, s32[1]{0:T(128)} %bitcast.3.refs_1_, bf16[4096,4096]{1,0:T(8,128)(2,1)} %refs_3_.5, bf16[4096,4096]{1,0:T(8,128)(2,1)} %refs_3_.5, bf16[4096,8192]{1,0:T(8,128)(2,1)} %refs_4_.5, bf16[256,8192]{1,0:T(8,128)(2,1)} %shard_map.60.refs_5_), custom_call_target="tpu_custom_call" | custom-call | flops 34359738368 | bytes 79691776 | tf_op jit(solution)/shard_map/pallas_call | solution.py:124
  205.3 152.5 %shard_map.62 = (bf16[1024,8192]{1,0:T(8,128)(2,1)}, bf16[1024,8192]{1,0:T(8,128)(2,1)}) custom-call(s32[1]{0:T(128)} %bitcast.refs_0_, s32[1]{0:T(128)} %bitcast.1.refs_1_, bf16[4096,4096]{1,0:T(8,128)(2,1)} %refs_3_.5, bf16[4096,4096]{1,0:T(8,128)(2,1)} %refs_3_.5, bf16[4096,8192]{1,0:T(8,128)(2,1)} %refs_4_.5, bf16[256,8192]{1,0:T(8,128)(2,1)} %get-tuple-element.43.refs_5_), custom_call_target="tpu_custom_call" | custom-call | flops 137438953472 | bytes 117440512 | tf_op jit(solution)/shard_map/pallas_call | solution.py:124
  357.8 0.0 collective-permute-start
  357.8 1.1 collective-permute-start.13
  358.9 42.0 %shard_map.63 = (bf16[128,8192]{1,0:T(8,128)(2,1)}, bf16[80,8192]{1,0:T(8,128)(2,1)}, bf16[32,8192]{1,0:T(8,128)(2,1)}, bf16[16,8192]{1,0:T(8,128)(2,1)}, bf16[1...) custom-call(s32[1]{0:T(128)} %bitcast.6.refs_0_, ...), custom_call_target="tpu_custom_call" | custom-call | flops 34359738368 | bytes 79691776 | tf_op jit(solution)/shard_map/pallas_call | solution.py:124
  400.9 1.0 collective-permute-start.6
  401.9 0.4 collective-permute-start.9
  402.2 1.0 collective-permute-start.8
  403.2 76.4 %collective-permute-done.6.refs_3_ = bf16[80,8192]{1,0:T(8,128)(2,1)S(1)} collective-permute-done((bf16[80,8192]{1,0:T(8,128)(2,1)}, bf16[80,8192]{1,0:T(8,128)(2,1)S(1)}, u32[]{:S(2)}, u32[]{:S(2)}) %collective-permute-start.6) | collective-permute-done | bytes 1310752 | tf_op jit(solution)/shard_map/ppermute | solution.py:257
  479.6 0.0 collective-permute-start.1
  479.6 43.6 %collective-permute-done.9.refs_4_ = bf16[128,8192]{1,0:T(8,128)(2,1)S(1)} collective-permute-done((bf16[128,8192]{1,0:T(8,128)(2,1)}, bf16[128,8192]{1,0:T(8,128)(2,1)S(1)}, u32[]{:S(2)}, u32[]{:S(2)}) %collective-permute-start.9) | collective-permute-done | bytes 2097184 | tf_op jit(solution)/shard_map/ppermute | solution.py:257
  523.2 1.0 collective-permute-start.12
  524.2 45.3 %collective-permute-done.8.refs_3_ = bf16[128,8192]{1,0:T(8,128)(2,1)S(1)} collective-permute-done((bf16[128,8192]{1,0:T(8,128)(2,1)}, bf16[128,8192]{1,0:T(8,128)(2,1)S(1)}, u32[]{:S(2)}, u32[]{:S(2)}) %collective-permute-start.8) | collective-permute-done | bytes 2097184 | tf_op jit(solution)/shard_map/ppermute | solution.py:257
  569.5 0.0 collective-permute-start.11
  569.5 0.0 collective-permute-done.13.refs_4_
  569.5 1.0 collective-permute-start.10
  570.5 87.5 %collective-permute-done.1.refs_4_ = bf16[256,8192]{1,0:T(8,128)(2,1)S(1)} collective-permute-done((bf16[256,8192]{1,0:T(8,128)(2,1)}, bf16[256,8192]{1,0:T(8,128)(2,1)S(1)}, u32[]{:S(2)}, u32[]{:S(2)}) %collective-permute-start.1) | collective-permute-done | bytes 4194336 | tf_op jit(solution)/shard_map/ppermute | solution.py:257
  658.0 1.8 collective-permute-start.7
  659.8 89.4 %collective-permute-done.12.refs_3_ = bf16[256,8192]{1,0:T(8,128)(2,1)S(1)} collective-permute-done((bf16[256,8192]{1,0:T(8,128)(2,1)}, bf16[256,8192]{1,0:T(8,128)(2,1)S(1)}, u32[]{:S(2)}, u32[]{:S(2)}) %collective-permute-start.12) | collective-permute-done | bytes 4194336 | tf_op jit(solution)/shard_map/ppermute | solution.py:257
  749.3 1.0 collective-permute-start.4
  750.3 87.5 %collective-permute-done.11.refs_4_ = bf16[256,8192]{1,0:T(8,128)(2,1)S(1)} collective-permute-done((bf16[256,8192]{1,0:T(8,128)(2,1)}, bf16[256,8192]{1,0:T(8,128)(2,1)S(1)}, u32[]{:S(2)}, u32[]{:S(2)}) %collective-permute-start.11) | collective-permute-done | bytes 4194336 | tf_op jit(solution)/shard_map/ppermute | solution.py:257
  837.8 1.8 collective-permute-start.5
  839.6 89.4 %collective-permute-done.10.refs_3_ = bf16[256,8192]{1,0:T(8,128)(2,1)S(1)} collective-permute-done((bf16[256,8192]{1,0:T(8,128)(2,1)}, bf16[256,8192]{1,0:T(8,128)(2,1)S(1)}, u32[]{:S(2)}, u32[]{:S(2)}) %collective-permute-start.10) | collective-permute-done | bytes 4194336 | tf_op jit(solution)/shard_map/ppermute | solution.py:257
  929.0 1.0 collective-permute-start.2
  930.1 0.9 copy-done.5
  931.0 1.6 copy-done.1
  932.6 19.0 %shard_map.64 = (f32[256,8192]{1,0:T(8,128)}, f32[256,128]{1,0:T(8,128)S(1)}) custom-call(bf16[1024,8192]{1,0:T(8,128)(2,1)} %refs_0_.13, bf16[1024,8192]{1,0:T(8,128)(2,1)} %get-tuple-element.44.refs_5_.refs_1_, bf16[1024,8192]{1,0:T(8,128)(2,1)} %collective-permute-done.refs_2_, bf16[256,8192]{1,0:T(8,128)(2,1)} %get-tuple-element.46.refs_3_, ...), custom_call_target="tpu_custom_call" | custom-call | flops 16777216 | bytes 29360128 | tf_op jit(solution)/shard_map/pallas_call | solution.py:186
  951.6 8.9 shard_map.65
  960.5 1.2 shard_map.66.refs_0_
  961.7 17.4 %shard_map.67 = (f32[256,8192]{1,0:T(8,128)}, f32[256,128]{1,0:T(8,128)S(1)}) custom-call(bf16[1024,8192]{1,0:T(8,128)(2,1)} %refs_0_.13, bf16[1024,8192]{1,0:T(8,128)(2,1)} %get-tuple-element.44.refs_5_.refs_1_, bf16[1024,8192]{1,0:T(8,128)(2,1)} %collective-permute-done.refs_2_, bf16[256,8192]{1,0:T(8,128)(2,1)} %copy-done.4, ...), custom_call_target="tpu_custom_call" | custom-call | flops 16777216 | bytes 29360128 | tf_op jit(solution)/shard_map/pallas_call | solution.py:186
  979.1 9.0 shard_map.68
  988.1 18.1 %shard_map.69 = (f32[256,8192]{1,0:T(8,128)}, f32[256,128]{1,0:T(8,128)S(1)}) custom-call(bf16[1024,8192]{1,0:T(8,128)(2,1)} %refs_0_.13, bf16[1024,8192]{1,0:T(8,128)(2,1)} %get-tuple-element.44.refs_5_.refs_1_, bf16[1024,8192]{1,0:T(8,128)(2,1)} %collective-permute-done.refs_2_, bf16[256,8192]{1,0:T(8,128)(2,1)} %copy-done.5, bf16[256,8192]{1,0:T(8,128)(2,1)} %copy-done.3, ...), custom_call_target="tpu_custom_call" | custom-call | flops 16777216 | bytes 29360128 | tf_op jit(solution)/shard_map/pallas_call | solution.py:186
  1006.2 9.0 shard_map.70
  1015.1 9.6 shard_map.71
  1024.8 4.8 shard_map.72
  1029.5 0.0 collective-permute-done.7.refs_4_
  1029.5 9.3 shard_map.73
  1038.8 1.7 copy-done
  1040.6 2.6 shard_map.74
  1043.2 5.0 shard_map.75
  1048.2 1.1 shard_map.76
  1049.3 0.0 collective-permute-done.2.refs_1_
  1049.3 0.0 collective-permute-done.3.refs_2_
  1049.3 4.7 shard_map.77
  1054.0 0.9 shard_map.78
  (17 shorter events, 0.0 us)
Async XLA Ops:
  357.8 572.3 %collective-permute-start = (bf16[1024,8192]{1,0:T(8,128)(2,1)}, bf16[1024,8192]{1,0:T(8,128)(2,1)}, u32[]{:S(2)}, u32[]{:S(2)}) collective-permute-start(bf16[1024,8192]{1,0:T(8,128)(2,1)} %get-tuple-element.45), channel_id=1, source_target_pairs={{0,1},{1,0},{2,3},{3,2},{4,5},{5,4},{6,7},{7,6}} | collective-permute-start | bytes 50331656 | tf_op jit(solution)/shard_map/ppermute | solution.py:257
  357.8 211.7 %collective-permute-start.13 = (bf16[256,8192]{1,0:T(8,128)(2,1)}, bf16[256,8192]{1,0:T(8,128)(2,1)}, u32[]{:S(2)}, u32[]{:S(2)}) collective-permute-start(bf16[256,8192]{1,0:T(8,128)(2,1)} %shard_map.60.refs_5_), channel_id=1, source_target_pairs={{0,3},{1,2},{2,1},{3,0},{4,7},{5,6},{6,5},{7,4}} | collective-permute-start | bytes 12582920 | tf_op jit(solution)/shard_map/ppermute | solution.py:257
  400.9 78.7 %collective-permute-start.6 = (bf16[80,8192]{1,0:T(8,128)(2,1)}, bf16[80,8192]{1,0:T(8,128)(2,1)S(1)}, u32[]{:S(2)}, u32[]{:S(2)}) collective-permute-start(bf16[80,8192]{1,0:T(8,128)(2,1)} %get-tuple-element.55), channel_id=1, source_target_pairs={{0,2},{1,3},{2,0},{3,1},{4,6},{5,7},{6,4},{7,5}} | collective-permute-start | bytes 3932168 | tf_op jit(solution)/shard_map/ppermute | solution.py:257
  401.9 121.3 %collective-permute-start.9 = (bf16[128,8192]{1,0:T(8,128)(2,1)}, bf16[128,8192]{1,0:T(8,128)(2,1)S(1)}, u32[]{:S(2)}, u32[]{:S(2)}) collective-permute-start(bf16[128,8192]{1,0:T(8,128)(2,1)} %get-tuple-element.57), channel_id=1, source_target_pairs={{0,3},{1,2},{2,1},{3,0},{4,7},{5,6},{6,5},{7,4}} | collective-permute-start | bytes 6291464 | tf_op jit(solution)/shard_map/ppermute | solution.py:257
  402.2 167.3 %collective-permute-start.8 = (bf16[128,8192]{1,0:T(8,128)(2,1)}, bf16[128,8192]{1,0:T(8,128)(2,1)S(1)}, u32[]{:S(2)}, u32[]{:S(2)}) collective-permute-start(bf16[128,8192]{1,0:T(8,128)(2,1)} %get-tuple-element.47.refs_5_), channel_id=1, source_target_pairs={{0,2},{1,3},{2,0},{3,1},{4,6},{5,7},{6,4},{7,5}} | collective-permute-start | bytes 6291464 | tf_op jit(solution)/shard_map/ppermute | solution.py:257
  479.6 178.4 %collective-permute-start.1 = (bf16[256,8192]{1,0:T(8,128)(2,1)}, bf16[256,8192]{1,0:T(8,128)(2,1)S(1)}, u32[]{:S(2)}, u32[]{:S(2)}) collective-permute-start(bf16[256,8192]{1,0:T(8,128)(2,1)} %shard_map.59.refs_3_), channel_id=1, source_target_pairs={{0,3},{1,2},{2,1},{3,0},{4,7},{5,6},{6,5},{7,4}} | collective-permute-start | bytes 12582920 | tf_op jit(solution)/shard_map/ppermute | solution.py:257
  523.2 428.4 %copy-start.7 = (bf16[128,8192]{1,0:T(8,128)(2,1)}, bf16[128,8192]{1,0:T(8,128)(2,1)S(1)}, u32[]{:S(2)}) copy-start(bf16[128,8192]{1,0:T(8,128)(2,1)S(1)} %collective-permute-done.9.refs_4_) | copy-start | bytes 6291460
  523.2 226.0 %collective-permute-start.12 = (bf16[256,8192]{1,0:T(8,128)(2,1)}, bf16[256,8192]{1,0:T(8,128)(2,1)S(1)}, u32[]{:S(2)}, u32[]{:S(2)}) collective-permute-start(bf16[256,8192]{1,0:T(8,128)(2,1)} %get-tuple-element.42.refs_3_), channel_id=1, source_target_pairs={{0,2},{1,3},{2,0},{3,1},{4,6},{5,7},{6,4},{7,5}} | collective-permute-start | bytes 12582920 | tf_op jit(solution)/shard_map/ppermute | solution.py:257
  569.5 268.3 %collective-permute-start.11 = (bf16[256,8192]{1,0:T(8,128)(2,1)}, bf16[256,8192]{1,0:T(8,128)(2,1)S(1)}, u32[]{:S(2)}, u32[]{:S(2)}) collective-permute-start(bf16[256,8192]{1,0:T(8,128)(2,1)} %get-tuple-element.58), channel_id=1, source_target_pairs={{0,3},{1,2},{2,1},{3,0},{4,7},{5,6},{6,5},{7,4}} | collective-permute-start | bytes 12582920 | tf_op jit(solution)/shard_map/ppermute | solution.py:257
  569.5 359.5 %collective-permute-start.10 = (bf16[256,8192]{1,0:T(8,128)(2,1)}, bf16[256,8192]{1,0:T(8,128)(2,1)S(1)}, u32[]{:S(2)}, u32[]{:S(2)}) collective-permute-start(bf16[256,8192]{1,0:T(8,128)(2,1)} %get-tuple-element.43.refs_5_), channel_id=1, source_target_pairs={{0,2},{1,3},{2,0},{3,1},{4,6},{5,7},{6,4},{7,5}} | collective-permute-start | bytes 12582920 | tf_op jit(solution)/shard_map/ppermute | solution.py:257
  658.0 272.0 %copy-start.6 = (bf16[256,8192]{1,0:T(8,128)(2,1)}, bf16[256,8192]{1,0:T(8,128)(2,1)S(1)}, u32[]{:S(2)}) copy-start(bf16[256,8192]{1,0:T(8,128)(2,1)S(1)} %collective-permute-done.1.refs_4_) | copy-start | bytes 12582916
  658.0 371.5 %collective-permute-start.7 = (bf16[80,8192]{1,0:T(8,128)(2,1)}, bf16[80,8192]{1,0:T(8,128)(2,1)S(1)}, u32[]{:S(2)}, u32[]{:S(2)}) collective-permute-start(bf16[80,8192]{1,0:T(8,128)(2,1)} %get-tuple-element.56), channel_id=1, source_target_pairs={{0,3},{1,2},{2,1},{3,0},{4,7},{5,6},{6,5},{7,4}} | collective-permute-start | bytes 3932168 | tf_op jit(solution)/shard_map/ppermute | solution.py:257
  749.3 180.8 %copy-start.4 = (bf16[256,8192]{1,0:T(8,128)(2,1)}, bf16[256,8192]{1,0:T(8,128)(2,1)S(1)}, u32[]{:S(2)}) copy-start(bf16[256,8192]{1,0:T(8,128)(2,1)S(1)} %collective-permute-done.12.refs_3_) | copy-start | bytes 12582916
  749.3 293.9 %collective-permute-start.4 = (bf16[32,8192]{1,0:T(8,128)(2,1)}, bf16[32,8192]{1,0:T(8,128)(2,1)}, u32[]{:S(2)}, u32[]{:S(2)}) collective-permute-start(bf16[32,8192]{1,0:T(8,128)(2,1)} %get-tuple-element.53), channel_id=1, source_target_pairs={{0,2},{1,3},{2,0},{3,1},{4,6},{5,7},{6,4},{7,5}} | collective-permute-start | bytes 1572872 | tf_op jit(solution)/shard_map/ppermute | solution.py:257
  837.8 113.8 %copy-start.3 = (bf16[256,8192]{1,0:T(8,128)(2,1)}, bf16[256,8192]{1,0:T(8,128)(2,1)S(1)}, u32[]{:S(2)}) copy-start(bf16[256,8192]{1,0:T(8,128)(2,1)S(1)} %collective-permute-done.11.refs_4_) | copy-start | bytes 12582916
  837.8 205.4 %collective-permute-start.5 = (bf16[32,8192]{1,0:T(8,128)(2,1)}, bf16[32,8192]{1,0:T(8,128)(2,1)}, u32[]{:S(2)}, u32[]{:S(2)}) collective-permute-start(bf16[32,8192]{1,0:T(8,128)(2,1)} %get-tuple-element.54), channel_id=1, source_target_pairs={{0,3},{1,2},{2,1},{3,0},{4,7},{5,6},{6,5},{7,4}} | collective-permute-start | bytes 1572872 | tf_op jit(solution)/shard_map/ppermute | solution.py:257
  929.0 2.0 copy-start.5
  929.0 120.3 %collective-permute-start.2 = (bf16[16,8192]{1,0:T(8,128)(2,1)}, bf16[16,8192]{1,0:T(8,128)(2,1)}, u32[]{:S(2)}, u32[]{:S(2)}) collective-permute-start(bf16[16,8192]{1,0:T(8,128)(2,1)} %get-tuple-element.51), channel_id=1, source_target_pairs={{0,2},{1,3},{2,0},{3,1},{4,6},{5,7},{6,4},{7,5}} | collective-permute-start | bytes 786440 | tf_op jit(solution)/shard_map/ppermute | solution.py:257
  930.1 119.2 %collective-permute-start.3 = (bf16[16,8192]{1,0:T(8,128)(2,1)}, bf16[16,8192]{1,0:T(8,128)(2,1)}, u32[]{:S(2)}, u32[]{:S(2)}) collective-permute-start(bf16[16,8192]{1,0:T(8,128)(2,1)} %get-tuple-element.52), channel_id=1, source_target_pairs={{0,3},{1,2},{2,1},{3,0},{4,7},{5,6},{6,5},{7,4}} | collective-permute-start | bytes 786440 | tf_op jit(solution)/shard_map/ppermute | solution.py:257
  931.0 1.6 copy-start.1
  932.6 19.0 %copy-start.2 = (f32[8192]{0:T(1024)S(1)}, f32[8192]{0:T(1024)}, u32[]{:S(2)}) copy-start(f32[8192]{0:T(1024)} %param.7) | copy-start | bytes 98308
  1038.8 1.7 copy-start

commit v6 on v5

--- a/solution.py
+++ b/solution.py
@@ -211,9 +211,9 @@
 
     return pl.pallas_call(
         body,
-        grid=(1,),
-        in_specs=[pl.BlockSpec((rows, cols), lambda i: (row0 // rows, 0))] * (1 + len(near)) + [ANY] * len(deps),
-        out_specs=pl.BlockSpec((rows, cols), lambda i: (0, 0)),
+        grid=(rows // 16,),
+        in_specs=[pl.BlockSpec((16, cols), lambda i: (row0 // 16 + i, 0))] * (1 + len(near)) + [ANY] * len(deps),
+        out_specs=pl.BlockSpec((16, cols), lambda i: (i, 0)),
         out_shape=jax.ShapeDtypeStruct((rows, cols), F32),
         compiler_params=pltpu.CompilerParams(vmem_limit_bytes=SMALL_VMEM),
         cost_estimate=pl.CostEstimate(flops=2 * rows * cols, bytes_accessed=10 * rows * cols, transcendentals=0),
@@ -287,9 +287,9 @@
         for c, (row, size) in enumerate(chunks):
             tr = 32 if (row | size) % 32 == 0 else 16
             if c == 1:
-                ready = near_sum(res, near, *chunks[-1], state[:1])
-            terms = (res, near) if c < len(chunks) - 1 else (ready, [])
-            h, sq = add_rows(*terms, pieces[row, size], row, size, tr, col_groups, state[:1] if state else dep, c)
+                ready = {k: near_sum(res, near, *chunks[k], state[:1]) for k in range(len(chunks) - 2, len(chunks))}
+            terms, step_rows = ((ready[c], []), size) if c >= len(chunks) - 2 else ((res, near), tr)
+            h, sq = add_rows(*terms, pieces[row, size], row, size, step_rows, col_groups, state[:1] if state else dep, c)
             state = norm_rows(h, sq, gain2, cols * col_groups, rows_total, row, tr, state)
         return tuple(state)
 

time: 1060 us -> 1060 us (level)
  no operation moved by 1% of the time
where the time goes in v6:
time: 1060 us
  Pallas kernels  522 us (49%)
  waiting for transfers between devices  518 us (49%)
  starting transfers between devices  11.2 us (1%)
    ppermute x14, waiting for transfers between devices, send(): return lax.ppermute(x, 'tp', [(i, i ^ flip) for i in range(tp)])  518 us
    pallas_call x5, Pallas kernels, products(): pl.pallas_call(body, grid_spec=pltpu.PrefetchScalarGridSpec(num_scalar_pr...  301 us
    pallas_call x1, Pallas kernels, head(): pl.pallas_call(body, grid=(2 * tiles,), in_specs=[pl.BlockSpec((HEAD_ROWS...  98.2 us
    pallas_call x7, Pallas kernels, add_rows(): pl.pallas_call(body, grid=(steps,), in_specs=in_specs, out_specs=[pl.Bloc...  83.5 us
    pallas_call x7, Pallas kernels, norm_rows(): pl.pallas_call(body, grid=(rows // tr,), in_specs=in_specs, out_specs=[pl...  36.3 us
  transfers between devices with their start and end apart: 14, of which 7 were waited for; matrix products, arithmetic and copies ran while one was open for 0% of the time, Pallas kernels for 15%

profile of v6, /device:TPU:0, one launch (start us, length us, event | category | flops | bytes accessed | tf_op | source)
XLA Modules:
  0.0 1057.0 jit_solution(17642969643843793837)
XLA Ops:
  0.6 98.2 %head.1 = (bf16[256,8192]{1,0:T(8,128)(2,1)}, bf16[256,8192]{1,0:T(8,128)(2,1)}) custom-call(bf16[4096,4096]{1,0:T(8,128)(2,1)} %refs_3_.5, bf16[4096,8192]{1,0:T(8,128)(2,1)} %refs_4_.5), custom_call_target="tpu_custom_call" | custom-call | flops 34359738368 | bytes 134217728 | tf_op jit(solution)/shard_map/head/pallas_call | solution.py:86
  98.9 32.3 %shard_map.59.refs_3_ = bf16[256,8192]{1,0:T(8,128)(2,1)} custom-call(s32[1]{0:T(128)} %bitcast.5.refs_0_, bf16[4096,4096]{1,0:T(8,128)(2,1)} %refs_3_.5, bf16[4096,8192]{1,0:T(8,128)(2,1)} %refs_4_.5, bf16[256,8192]{1,0:T(8,128)(2,1)} %get-tuple-element.42.refs_3_), custom_call_target="tpu_custom_call" | custom-call | flops 17179869184 | bytes 73400320 | tf_op jit(solution)/shard_map/pallas_call | solution.py:124
  131.1 32.3 %shard_map.60.refs_5_ = bf16[256,8192]{1,0:T(8,128)(2,1)} custom-call(s32[1]{0:T(128)} %bitcast.4.refs_0_, bf16[4096,4096]{1,0:T(8,128)(2,1)} %refs_3_.5, bf16[4096,8192]{1,0:T(8,128)(2,1)} %refs_4_.5, bf16[256,8192]{1,0:T(8,128)(2,1)} %shard_map.59.refs_3_), custom_call_target="tpu_custom_call" | custom-call | flops 17179869184 | bytes 73400320 | tf_op jit(solution)/shard_map/pallas_call | solution.py:124
  163.4 42.0 %shard_map.61 = (bf16[256,8192]{1,0:T(8,128)(2,1)}, bf16[256,8192]{1,0:T(8,128)(2,1)}) custom-call(s32[1]{0:T(128)} %bitcast.2.refs_0_, s32[1]{0:T(128)} %bitcast.3.refs_1_, bf16[4096,4096]{1,0:T(8,128)(2,1)} %refs_3_.5, bf16[4096,4096]{1,0:T(8,128)(2,1)} %refs_3_.5, bf16[4096,8192]{1,0:T(8,128)(2,1)} %refs_4_.5, bf16[256,8192]{1,0:T(8,128)(2,1)} %shard_map.60.refs_5_), custom_call_target="tpu_custom_call" | custom-call | flops 34359738368 | bytes 79691776 | tf_op jit(solution)/shard_map/pallas_call | solution.py:124
  205.4 152.5 %shard_map.62 = (bf16[1024,8192]{1,0:T(8,128)(2,1)}, bf16[1024,8192]{1,0:T(8,128)(2,1)}) custom-call(s32[1]{0:T(128)} %bitcast.refs_0_, s32[1]{0:T(128)} %bitcast.1.refs_1_, bf16[4096,4096]{1,0:T(8,128)(2,1)} %refs_3_.5, bf16[4096,4096]{1,0:T(8,128)(2,1)} %refs_3_.5, bf16[4096,8192]{1,0:T(8,128)(2,1)} %refs_4_.5, bf16[256,8192]{1,0:T(8,128)(2,1)} %get-tuple-element.43.refs_5_), custom_call_target="tpu_custom_call" | custom-call | flops 137438953472 | bytes 117440512 | tf_op jit(solution)/shard_map/pallas_call | solution.py:124
  357.9 0.0 collective-permute-start
  357.9 1.1 collective-permute-start.13
  359.0 42.0 %shard_map.63 = (bf16[128,8192]{1,0:T(8,128)(2,1)}, bf16[80,8192]{1,0:T(8,128)(2,1)}, bf16[32,8192]{1,0:T(8,128)(2,1)}, bf16[16,8192]{1,0:T(8,128)(2,1)}, bf16[1...) custom-call(s32[1]{0:T(128)} %bitcast.6.refs_0_, ...), custom_call_target="tpu_custom_call" | custom-call | flops 34359738368 | bytes 79691776 | tf_op jit(solution)/shard_map/pallas_call | solution.py:124
  401.0 1.0 collective-permute-start.6
  402.1 0.4 collective-permute-start.9
  402.4 1.0 collective-permute-start.8
  403.4 76.3 %collective-permute-done.6.refs_3_ = bf16[80,8192]{1,0:T(8,128)(2,1)S(1)} collective-permute-done((bf16[80,8192]{1,0:T(8,128)(2,1)}, bf16[80,8192]{1,0:T(8,128)(2,1)S(1)}, u32[]{:S(2)}, u32[]{:S(2)}) %collective-permute-start.6) | collective-permute-done | bytes 1310752 | tf_op jit(solution)/shard_map/ppermute | solution.py:257
  479.7 1.1 copy-done.3
  480.8 0.0 collective-permute-start.1
  480.8 42.5 %collective-permute-done.9.refs_4_ = bf16[128,8192]{1,0:T(8,128)(2,1)S(1)} collective-permute-done((bf16[128,8192]{1,0:T(8,128)(2,1)}, bf16[128,8192]{1,0:T(8,128)(2,1)S(1)}, u32[]{:S(2)}, u32[]{:S(2)}) %collective-permute-start.9) | collective-permute-done | bytes 2097184 | tf_op jit(solution)/shard_map/ppermute | solution.py:257
  523.3 1.0 collective-permute-start.12
  524.3 45.3 %collective-permute-done.8.refs_3_ = bf16[128,8192]{1,0:T(8,128)(2,1)S(1)} collective-permute-done((bf16[128,8192]{1,0:T(8,128)(2,1)}, bf16[128,8192]{1,0:T(8,128)(2,1)S(1)}, u32[]{:S(2)}, u32[]{:S(2)}) %collective-permute-start.8) | collective-permute-done | bytes 2097184 | tf_op jit(solution)/shard_map/ppermute | solution.py:257
  569.6 0.0 collective-permute-done.13.refs_4_
  569.6 1.0 collective-permute-start.10
  570.7 87.5 %collective-permute-done.1.refs_4_ = bf16[256,8192]{1,0:T(8,128)(2,1)S(1)} collective-permute-done((bf16[256,8192]{1,0:T(8,128)(2,1)}, bf16[256,8192]{1,0:T(8,128)(2,1)S(1)}, u32[]{:S(2)}, u32[]{:S(2)}) %collective-permute-start.1) | collective-permute-done | bytes 4194336 | tf_op jit(solution)/shard_map/ppermute | solution.py:257
  658.2 1.8 collective-permute-start.7
  660.0 89.4 %collective-permute-done.12.refs_3_ = bf16[256,8192]{1,0:T(8,128)(2,1)S(1)} collective-permute-done((bf16[256,8192]{1,0:T(8,128)(2,1)}, bf16[256,8192]{1,0:T(8,128)(2,1)S(1)}, u32[]{:S(2)}, u32[]{:S(2)}) %collective-permute-start.12) | collective-permute-done | bytes 4194336 | tf_op jit(solution)/shard_map/ppermute | solution.py:257
  749.4 1.0 collective-permute-start.4
  750.4 87.5 %collective-permute-done.11.refs_4_ = bf16[256,8192]{1,0:T(8,128)(2,1)S(1)} collective-permute-done((bf16[256,8192]{1,0:T(8,128)(2,1)}, bf16[256,8192]{1,0:T(8,128)(2,1)S(1)}, u32[]{:S(2)}, u32[]{:S(2)}) %collective-permute-start.11) | collective-permute-done | bytes 4194336 | tf_op jit(solution)/shard_map/ppermute | solution.py:257
  837.9 1.8 collective-permute-start.5
  839.7 89.4 %collective-permute-done.10.refs_3_ = bf16[256,8192]{1,0:T(8,128)(2,1)S(1)} collective-permute-done((bf16[256,8192]{1,0:T(8,128)(2,1)}, bf16[256,8192]{1,0:T(8,128)(2,1)S(1)}, u32[]{:S(2)}, u32[]{:S(2)}) %collective-permute-start.10) | collective-permute-done | bytes 4194336 | tf_op jit(solution)/shard_map/ppermute | solution.py:257
  929.2 1.0 collective-permute-start.2
  930.2 0.0 collective-permute-done.refs_2_
  930.2 0.0 collective-permute-start.3
  930.2 1.0 copy-done.7
  931.2 1.6 copy-done.1
  932.8 19.0 %shard_map.64 = (f32[256,8192]{1,0:T(8,128)}, f32[256,128]{1,0:T(8,128)S(1)}) custom-call(bf16[1024,8192]{1,0:T(8,128)(2,1)} %refs_0_.13, bf16[1024,8192]{1,0:T(8,128)(2,1)} %get-tuple-element.44.refs_5_.refs_1_, bf16[1024,8192]{1,0:T(8,128)(2,1)} %collective-permute-done.refs_2_, bf16[256,8192]{1,0:T(8,128)(2,1)} %get-tuple-element.46.refs_3_, ...), custom_call_target="tpu_custom_call" | custom-call | flops 16777216 | bytes 29360128 | tf_op jit(solution)/shard_map/pallas_call | solution.py:186
  951.8 8.9 shard_map.65
  960.7 1.2 shard_map.66.refs_0_
  961.9 1.5 shard_map.67.refs_0_
  963.4 17.5 %shard_map.68 = (f32[256,8192]{1,0:T(8,128)}, f32[256,128]{1,0:T(8,128)S(1)}) custom-call(bf16[1024,8192]{1,0:T(8,128)(2,1)} %refs_0_.13, bf16[1024,8192]{1,0:T(8,128)(2,1)} %get-tuple-element.44.refs_5_.refs_1_, bf16[1024,8192]{1,0:T(8,128)(2,1)} %collective-permute-done.refs_2_, bf16[256,8192]{1,0:T(8,128)(2,1)} %copy-done.6, ...), custom_call_target="tpu_custom_call" | custom-call | flops 16777216 | bytes 29360128 | tf_op jit(solution)/shard_map/pallas_call | solution.py:186
  980.9 9.0 shard_map.69
  989.8 18.1 %shard_map.70 = (f32[256,8192]{1,0:T(8,128)}, f32[256,128]{1,0:T(8,128)S(1)}) custom-call(bf16[1024,8192]{1,0:T(8,128)(2,1)} %refs_0_.13, bf16[1024,8192]{1,0:T(8,128)(2,1)} %get-tuple-element.44.refs_5_.refs_1_, bf16[1024,8192]{1,0:T(8,128)(2,1)} %collective-permute-done.refs_2_, bf16[256,8192]{1,0:T(8,128)(2,1)} %copy-done.7, bf16[256,8192]{1,0:T(8,128)(2,1)} %copy-done.5, ...), custom_call_target="tpu_custom_call" | custom-call | flops 16777216 | bytes 29360128 | tf_op jit(solution)/shard_map/pallas_call | solution.py:186
  1007.9 9.0 shard_map.71
  1016.8 9.7 shard_map.72
  1026.5 4.9 shard_map.73
  1031.4 9.6 shard_map.74
  1041.0 1.7 copy-done
  1042.8 2.6 shard_map.75
  1045.4 5.0 shard_map.76
  1050.3 1.1 shard_map.77
  1051.4 4.7 shard_map.78
  1056.1 0.9 shard_map.79
  (22 shorter events, 0.0 us)
Async XLA Ops:
  357.9 572.3 %collective-permute-start = (bf16[1024,8192]{1,0:T(8,128)(2,1)}, bf16[1024,8192]{1,0:T(8,128)(2,1)}, u32[]{:S(2)}, u32[]{:S(2)}) collective-permute-start(bf16[1024,8192]{1,0:T(8,128)(2,1)} %get-tuple-element.45), channel_id=1, source_target_pairs={{0,1},{1,0},{2,3},{3,2},{4,5},{5,4},{6,7},{7,6}} | collective-permute-start | bytes 50331656 | tf_op jit(solution)/shard_map/ppermute | solution.py:257
  357.9 211.7 %collective-permute-start.13 = (bf16[256,8192]{1,0:T(8,128)(2,1)}, bf16[256,8192]{1,0:T(8,128)(2,1)}, u32[]{:S(2)}, u32[]{:S(2)}) collective-permute-start(bf16[256,8192]{1,0:T(8,128)(2,1)} %shard_map.60.refs_5_), channel_id=1, source_target_pairs={{0,3},{1,2},{2,1},{3,0},{4,7},{5,6},{6,5},{7,4}} | collective-permute-start | bytes 12582920 | tf_op jit(solution)/shard_map/ppermute | solution.py:257
  401.0 78.7 %collective-permute-start.6 = (bf16[80,8192]{1,0:T(8,128)(2,1)}, bf16[80,8192]{1,0:T(8,128)(2,1)S(1)}, u32[]{:S(2)}, u32[]{:S(2)}) collective-permute-start(bf16[80,8192]{1,0:T(8,128)(2,1)} %get-tuple-element.55), channel_id=1, source_target_pairs={{0,2},{1,3},{2,0},{3,1},{4,6},{5,7},{6,4},{7,5}} | collective-permute-start | bytes 3932168 | tf_op jit(solution)/shard_map/ppermute | solution.py:257
  402.1 121.3 %collective-permute-start.9 = (bf16[128,8192]{1,0:T(8,128)(2,1)}, bf16[128,8192]{1,0:T(8,128)(2,1)S(1)}, u32[]{:S(2)}, u32[]{:S(2)}) collective-permute-start(bf16[128,8192]{1,0:T(8,128)(2,1)} %get-tuple-element.57), channel_id=1, source_target_pairs={{0,3},{1,2},{2,1},{3,0},{4,7},{5,6},{6,5},{7,4}} | collective-permute-start | bytes 6291464 | tf_op jit(solution)/shard_map/ppermute | solution.py:257
  402.4 167.2 %collective-permute-start.8 = (bf16[128,8192]{1,0:T(8,128)(2,1)}, bf16[128,8192]{1,0:T(8,128)(2,1)S(1)}, u32[]{:S(2)}, u32[]{:S(2)}) collective-permute-start(bf16[128,8192]{1,0:T(8,128)(2,1)} %get-tuple-element.47.refs_5_), channel_id=1, source_target_pairs={{0,2},{1,3},{2,0},{3,1},{4,6},{5,7},{6,4},{7,5}} | collective-permute-start | bytes 6291464 | tf_op jit(solution)/shard_map/ppermute | solution.py:257
  479.7 1.1 copy-start.3
  480.8 177.3 %collective-permute-start.1 = (bf16[256,8192]{1,0:T(8,128)(2,1)}, bf16[256,8192]{1,0:T(8,128)(2,1)S(1)}, u32[]{:S(2)}, u32[]{:S(2)}) collective-permute-start(bf16[256,8192]{1,0:T(8,128)(2,1)} %shard_map.59.refs_3_), channel_id=1, source_target_pairs={{0,3},{1,2},{2,1},{3,0},{4,7},{5,6},{6,5},{7,4}} | collective-permute-start | bytes 12582920 | tf_op jit(solution)/shard_map/ppermute | solution.py:257
  523.3 46.3 %copy-start.9 = (bf16[128,8192]{1,0:T(8,128)(2,1)}, bf16[128,8192]{1,0:T(8,128)(2,1)S(1)}, u32[]{:S(2)}) copy-start(bf16[128,8192]{1,0:T(8,128)(2,1)S(1)} %collective-permute-done.9.refs_4_) | copy-start | bytes 6291460
  523.3 226.1 %collective-permute-start.12 = (bf16[256,8192]{1,0:T(8,128)(2,1)}, bf16[256,8192]{1,0:T(8,128)(2,1)S(1)}, u32[]{:S(2)}, u32[]{:S(2)}) collective-permute-start(bf16[256,8192]{1,0:T(8,128)(2,1)} %get-tuple-element.42.refs_3_), channel_id=1, source_target_pairs={{0,2},{1,3},{2,0},{3,1},{4,6},{5,7},{6,4},{7,5}} | collective-permute-start | bytes 12582920 | tf_op jit(solution)/shard_map/ppermute | solution.py:257
  569.6 268.3 %collective-permute-start.11 = (bf16[256,8192]{1,0:T(8,128)(2,1)}, bf16[256,8192]{1,0:T(8,128)(2,1)S(1)}, u32[]{:S(2)}, u32[]{:S(2)}) collective-permute-start(bf16[256,8192]{1,0:T(8,128)(2,1)} %get-tuple-element.58), channel_id=1, source_target_pairs={{0,3},{1,2},{2,1},{3,0},{4,7},{5,6},{6,5},{7,4}} | collective-permute-start | bytes 12582920 | tf_op jit(solution)/shard_map/ppermute | solution.py:257
  569.6 359.5 %collective-permute-start.10 = (bf16[256,8192]{1,0:T(8,128)(2,1)}, bf16[256,8192]{1,0:T(8,128)(2,1)S(1)}, u32[]{:S(2)}, u32[]{:S(2)}) collective-permute-start(bf16[256,8192]{1,0:T(8,128)(2,1)} %get-tuple-element.43.refs_5_), channel_id=1, source_target_pairs={{0,2},{1,3},{2,0},{3,1},{4,6},{5,7},{6,4},{7,5}} | collective-permute-start | bytes 12582920 | tf_op jit(solution)/shard_map/ppermute | solution.py:257
  658.2 272.0 %copy-start.8 = (bf16[256,8192]{1,0:T(8,128)(2,1)}, bf16[256,8192]{1,0:T(8,128)(2,1)S(1)}, u32[]{:S(2)}) copy-start(bf16[256,8192]{1,0:T(8,128)(2,1)S(1)} %collective-permute-done.1.refs_4_) | copy-start | bytes 12582916
  658.2 373.2 %collective-permute-start.7 = (bf16[80,8192]{1,0:T(8,128)(2,1)}, bf16[80,8192]{1,0:T(8,128)(2,1)}, u32[]{:S(2)}, u32[]{:S(2)}) collective-permute-start(bf16[80,8192]{1,0:T(8,128)(2,1)} %get-tuple-element.56), channel_id=1, source_target_pairs={{0,3},{1,2},{2,1},{3,0},{4,7},{5,6},{6,5},{7,4}} | collective-permute-start | bytes 3932168 | tf_op jit(solution)/shard_map/ppermute | solution.py:257
  749.4 202.3 %copy-start.6 = (bf16[256,8192]{1,0:T(8,128)(2,1)}, bf16[256,8192]{1,0:T(8,128)(2,1)S(1)}, u32[]{:S(2)}) copy-start(bf16[256,8192]{1,0:T(8,128)(2,1)S(1)} %collective-permute-done.12.refs_3_) | copy-start | bytes 12582916
  749.4 296.0 %collective-permute-start.4 = (bf16[32,8192]{1,0:T(8,128)(2,1)}, bf16[32,8192]{1,0:T(8,128)(2,1)}, u32[]{:S(2)}, u32[]{:S(2)}) collective-permute-start(bf16[32,8192]{1,0:T(8,128)(2,1)} %get-tuple-element.53), channel_id=1, source_target_pairs={{0,2},{1,3},{2,0},{3,1},{4,6},{5,7},{6,4},{7,5}} | collective-permute-start | bytes 1572872 | tf_op jit(solution)/shard_map/ppermute | solution.py:257
  837.9 113.8 %copy-start.5 = (bf16[256,8192]{1,0:T(8,128)(2,1)}, bf16[256,8192]{1,0:T(8,128)(2,1)S(1)}, u32[]{:S(2)}) copy-start(bf16[256,8192]{1,0:T(8,128)(2,1)S(1)} %collective-permute-done.11.refs_4_) | copy-start | bytes 12582916
  837.9 207.4 %collective-permute-start.5 = (bf16[32,8192]{1,0:T(8,128)(2,1)}, bf16[32,8192]{1,0:T(8,128)(2,1)}, u32[]{:S(2)}, u32[]{:S(2)}) collective-permute-start(bf16[32,8192]{1,0:T(8,128)(2,1)} %get-tuple-element.54), channel_id=1, source_target_pairs={{0,3},{1,2},{2,1},{3,0},{4,7},{5,6},{6,5},{7,4}} | collective-permute-start | bytes 1572872 | tf_op jit(solution)/shard_map/ppermute | solution.py:257
  929.2 2.0 copy-start.7
  929.2 122.3 %collective-permute-start.2 = (bf16[16,8192]{1,0:T(8,128)(2,1)}, bf16[16,8192]{1,0:T(8,128)(2,1)}, u32[]{:S(2)}, u32[]{:S(2)}) collective-permute-start(bf16[16,8192]{1,0:T(8,128)(2,1)} %get-tuple-element.51), channel_id=1, source_target_pairs={{0,2},{1,3},{2,0},{3,1},{4,6},{5,7},{6,4},{7,5}} | collective-permute-start | bytes 786440 | tf_op jit(solution)/shard_map/ppermute | solution.py:257
  930.2 121.2 %collective-permute-start.3 = (bf16[16,8192]{1,0:T(8,128)(2,1)}, bf16[16,8192]{1,0:T(8,128)(2,1)}, u32[]{:S(2)}, u32[]{:S(2)}) collective-permute-start(bf16[16,8192]{1,0:T(8,128)(2,1)} %get-tuple-element.52), channel_id=1, source_target_pairs={{0,3},{1,2},{2,1},{3,0},{4,7},{5,6},{6,5},{7,4}} | collective-permute-start | bytes 786440 | tf_op jit(solution)/shard_map/ppermute | solution.py:257
  931.2 1.6 copy-start.1
  932.7 19.0 %copy-start.2 = (f32[8192]{0:T(1024)S(1)}, f32[8192]{0:T(1024)}, u32[]{:S(2)}) copy-start(f32[8192]{0:T(1024)} %param.7) | copy-start | bytes 98308
  1026.5 4.9 copy-start.4
  1041.0 1.7 copy-start
